TPU v7x, 512 devices: a whole 4x8x8 slice. The times are simulated.
512 devices in a mesh: gx: 8 (over z_lo, core), yz: 64 (over z_hi, y, x).
Axes of the slice: x: 4, y: 8, z: 8 (z_hi: 2, z_lo: 4; z = z_hi * 4 + z_lo), core: 2. Of those that a mesh axis runs over, the one named last changes fastest.
Arguments:
- features_in: bfloat16 [64, 32, 96, 144], P('yz', None, 'gx'), may hold values from -6 to 6
- encode_fine_first: bfloat16 [32, 864], replicated, may hold values from -0.3125 to 0.3125
- encode_fine_second: bfloat16 [32, 864], replicated, may hold values from -0.3125 to 0.3125
- reduce_fine: bfloat16 [64, 256], replicated, may hold values from -0.5 to 0.5
- encode_middle_first: bfloat16 [64, 1728], replicated, may hold values from -0.21875 to 0.21875
- encode_middle_second: bfloat16 [64, 1728], replicated, may hold values from -0.21875 to 0.21875
- reduce_middle: bfloat16 [256, 512], replicated, may hold values from -0.375 to 0.375
- bottom_first: bfloat16 [1024, 1728], P('yz'), may hold values from -0.109375 to 0.109375
- bottom_second: bfloat16 [1024, 1728], P('yz'), may hold values from -0.109375 to 0.109375
- expand_middle: bfloat16 [256, 512], replicated, may hold values from -0.5 to 0.5
- decode_middle_first: bfloat16 [64, 1728], replicated, may hold values from -0.21875 to 0.21875
- decode_middle_second: bfloat16 [64, 1728], replicated, may hold values from -0.21875 to 0.21875
- expand_fine: bfloat16 [64, 256], replicated, may hold values from -1 to 1
- decode_fine_first: bfloat16 [32, 864], replicated, may hold values from -0.3125 to 0.3125
- decode_fine_second: bfloat16 [32, 864], replicated, may hold values from -0.3125 to 0.3125
Outputs:
- features_out: bfloat16 [64, 32, 96, 144], P('yz', None, 'gx')
All inputs are finite; a program needn't handle non-finite values.
Results may differ from a plain program's by a relative error of at most 0.023.
Values may be sent and summed in bfloat16 or wider, within the bound.
A program may use at most 128 MiB of HBM per device.

v0:
```python
import math

import jax
import jax.numpy as jnp
from jax import lax
from jax.sharding import PartitionSpec as P


def with_halo(cells, sides, width):
    for axis, dim in sides:
        count = lax.axis_size(axis)
        head = lax.slice_in_dim(cells, 0, width, axis=dim)
        tail = lax.slice_in_dim(cells, cells.shape[dim] - width, cells.shape[dim], axis=dim)
        cells = jnp.concatenate(
            [
                lax.ppermute(tail, axis, [(i, (i + 1) % count) for i in range(count)]),
                cells,
                lax.ppermute(head, axis, [((i + 1) % count, i) for i in range(count)]),
            ],
            axis=dim,
        )
    return cells


def shortened(x):
    return jax.tree.map(lambda a: a.astype(jnp.bfloat16) if a.dtype == jnp.float32 else a, x)


def from_behind(block, axis, distance):
    devices = range(lax.axis_size(axis))
    route = [((i - distance) % len(devices), i) for i in devices]
    return lax.ppermute(block, axis, route)


def conv_taps(padded, weight, width_in):
    kernel = weight.reshape(weight.shape[0], width_in, 3, 3, 3)
    return lax.conv_general_dilated(
        padded[None],
        kernel,
        (1, 1, 1),
        "VALID",
        dimension_numbers=("NCDHW", "OIDHW", "NCDHW"),
        preferred_element_type=jnp.float32,
    )[0]


def rectify(running):
    return jnp.maximum(running, 0.0).astype(jnp.bfloat16)


def shrink(region, weight):
    kernel = weight.reshape(weight.shape[0], region.shape[0], 2, 2, 2)
    result = lax.conv_general_dilated(
        region[None],
        kernel,
        (2, 2, 2),
        "VALID",
        dimension_numbers=("NCDHW", "OIDHW", "NCDHW"),
        preferred_element_type=jnp.float32,
    )[0]
    return result.astype(jnp.bfloat16)


def expand(region, weight, skipped):
    width_in, extent_x, extent_y, extent_z = region.shape
    width_out = weight.shape[1] // 8
    columns = lax.dot_general(
        weight,
        region.reshape(width_in, -1),
        (((0,), (0,)), ((), ())),
        preferred_element_type=jnp.float32,
    )
    spread = columns.reshape(width_out, 2, 2, 2, extent_x, extent_y, extent_z).transpose(
        0, 4, 1, 5, 2, 6, 3
    )
    spread = spread.reshape(width_out, 2 * extent_x, 2 * extent_y, 2 * extent_z)
    return (spread + skipped.astype(jnp.float32)).astype(jnp.bfloat16)


def x_margins(region):
    return with_halo(region, (("gx", 1),), 1)


def from_peer(plane, offset):
    return from_behind(shortened(plane), "yz", offset).astype(plane.dtype)


def pad_block(region, across):
    extended = x_margins(region)
    below_face = from_peer(extended[:, :, -1:, :], across)
    above_face = from_peer(extended[:, :, :1, :], -across)
    extended = jnp.concatenate([below_face, extended, above_face], axis=2)
    column = lax.axis_index("yz") % across
    last_plane = extended[:, :, :, -1:]
    first_plane = extended[:, :, :, :1]
    behind = jnp.where(column == 0, from_peer(last_plane, 1 - across), from_peer(last_plane, 1))
    ahead = jnp.where(
        column == across - 1, from_peer(first_plane, across - 1), from_peer(first_plane, -1)
    )
    return jnp.concatenate([behind, extended, ahead], axis=3)


def conv_layer(region, weight, across):
    return rectify(conv_taps(pad_block(region, across), weight, region.shape[0]))


def assemble(stored):
    width_out = stored.shape[0] // 4
    return (
        stored.reshape(4, width_out, stored.shape[1])
        .transpose(1, 0, 2)
        .reshape(width_out, 4 * stored.shape[1])
    )


def bottom_layer(region, weight, across):
    width_in = region.shape[0]
    padded = pad_block(region, across)
    gathered = lax.all_gather(weight, "yz", axis=0, tiled=True)
    return rectify(conv_taps(padded, assemble(gathered), width_in))


def body(
    features_in,
    encode_fine_first,
    encode_fine_second,
    reduce_fine,
    encode_middle_first,
    encode_middle_second,
    reduce_middle,
    bottom_first,
    bottom_second,
    expand_middle,
    decode_middle_first,
    decode_middle_second,
    expand_fine,
    decode_fine_first,
    decode_fine_second,
):
    across = math.isqrt(lax.axis_size("yz"))
    width_fine, extent = (features_in.shape[1], features_in.shape[2])
    region = features_in.reshape(width_fine, extent, extent, extent)
    fine_skip = conv_layer(
        conv_layer(region, encode_fine_first, across), encode_fine_second, across
    )
    middle = shrink(fine_skip, reduce_fine)
    middle_skip = conv_layer(
        conv_layer(middle, encode_middle_first, across), encode_middle_second, across
    )
    bottom = shrink(middle_skip, reduce_middle)
    bottom = bottom_layer(bottom_layer(bottom, bottom_first, across), bottom_second, across)
    rising = expand(bottom, expand_middle, middle_skip)
    rising = conv_layer(
        conv_layer(rising, decode_middle_first, across), decode_middle_second, across
    )
    rising = expand(rising, expand_fine, fine_skip)
    rising = conv_layer(conv_layer(rising, decode_fine_first, across), decode_fine_second, across)
    return rising.reshape(1, width_fine, extent, extent * extent)


def solution(mesh):
    placed = (
        P("yz", None, "gx", None),
        P(),
        P(),
        P(),
        P(),
        P(),
        P(),
        P("yz", None),
        P("yz", None),
        P(),
        P(),
        P(),
        P(),
        P(),
        P(),
    )
    return jax.shard_map(
        body, mesh=mesh, in_specs=placed, out_specs=P("yz", None, "gx", None), check_vma=False
    )
```

profile of v0, /device:TPU:62, one launch (start us, length us, event | category | flops | bytes accessed | tf_op | source)
XLA Modules:
  0.0 663.7 jit_solution(2394427697510291306)
XLA Ops:
  10.6 7.3 %collective-permute-start.1 = (bf16[32,1,12,12]{0,3,2,1:T(8,128)(2,1)S(1)}, bf16[32,1,12,12]{0,3,2,1:T(8,128)(2,1)S(1)}, u32[]{:S(2)}, u32[]{:S(2)}) collective-permute-start(bf16[32,1,12,12]{0,3,2,1:T(8,128)(2,1)S(1)} %get-tuple-element.27), channel_id=1, source_target_pairs={{64,0},{128,64},{192,128},{256,192},{320,256},{384,320},{448,384},... | collective-permute-start | bytes 27656 | tf_op jit(solution)/shard_map/ppermute | solution.py:18
  19.7 9.2 %collective-permute-start.2 = (bf16[32,14,1,12]{0,3,2,1:T(8,128)(2,1)S(1)}, bf16[32,14,1,12]{0,3,2,1:T(8,128)(2,1)S(1)}, u32[]{:S(2)}, u32[]{:S(2)}) collective-permute-start(bf16[32,14,1,12]{0,3,2,1:T(8,128)(2,1)S(1)} %get-tuple-element.19), channel_id=1, source_target_pairs={{56,0},{57,1},{58,2},{59,3},{60,4},{61,5},{62,6},{63,7},{0,8},{1,9... | collective-permute-start | bytes 32264 | tf_op jit(solution)/shard_map/ppermute | solution.py:32
  31.2 11.2 %collective-permute-done.3 = bf16[32,14,1,12]{0,3,2,1:T(8,128)(2,1)S(1)} collective-permute-done((bf16[32,14,1,12]{0,3,2,1:T(8,128)(2,1)S(1)}, bf16[32,14,1,12]{0,3,2,1:T(8,128)(2,1)S(1)}, u32[]{:S(2)}, u32[]{:S(2)}) %collective-permute-start.3) | collective-permute-done | bytes 10784 | tf_op jit(solution)/shard_map/ppermute | solution.py:32
  45.4 10.3 %collective-permute-start.5 = (bf16[32,14,14,1]{0,3,2,1:T(2,128)(2,1)S(1)}, bf16[32,14,14,1]{0,3,2,1:T(2,128)(2,1)S(1)}, u32[]{:S(2)}, u32[]{:S(2)}) collective-permute-start(bf16[32,14,14,1]{0,3,2,1:T(2,128)(2,1)S(1)} %get-tuple-element.11), channel_id=1, source_target_pairs={{63,0},{0,1},{1,2},{2,3},{3,4},{4,5},{5,6},{6,7},{7,8},{8,9},{9,10... | collective-permute-start | bytes 37640 | tf_op jit(solution)/shard_map/ppermute | solution.py:32
  64.7 9.4 %collective-permute-done.7 = bf16[32,14,14,1]{0,3,2,1:T(2,128)(2,1)S(1)} collective-permute-done((bf16[32,14,14,1]{0,3,2,1:T(2,128)(2,1)S(1)}, bf16[32,14,14,1]{0,3,2,1:T(2,128)(2,1)S(1)}, u32[]{:S(2)}, u32[]{:S(2)}) %collective-permute-start.7) | collective-permute-done | bytes 12576 | tf_op jit(solution)/shard_map/ppermute | solution.py:32
  97.1 8.0 %collective-permute-done.11 = bf16[32,14,1,12]{0,3,2,1:T(8,128)(2,1)S(1)} collective-permute-done((bf16[32,14,1,12]{0,3,2,1:T(8,128)(2,1)S(1)}, bf16[32,14,1,12]{0,3,2,1:T(8,128)(2,1)S(1)}, u32[]{:S(2)}, u32[]{:S(2)}) %collective-permute-start.11) | collective-permute-done | bytes 10784 | tf_op jit(solution)/shard_map/ppermute | solution.py:32
  107.6 10.0 %collective-permute-start.13 = (bf16[32,14,14,1]{0,3,2,1:T(2,128)(2,1)S(1)}, bf16[32,14,14,1]{0,3,2,1:T(2,128)(2,1)S(1)}, u32[]{:S(2)}, u32[]{:S(2)}) collective-permute-start(bf16[32,14,14,1]{0,3,2,1:T(2,128)(2,1)S(1)} %get-tuple-element.9), channel_id=1, source_target_pairs={{63,0},{0,1},{1,2},{2,3},{3,4},{4,5},{5,6},{6,7},{7,8},{8,9},{9,10... | collective-permute-start | bytes 37640 | tf_op jit(solution)/shard_map/ppermute | solution.py:32
  126.7 10.4 %collective-permute-done.15 = bf16[32,14,14,1]{0,3,2,1:T(2,128)(2,1)S(1)} collective-permute-done((bf16[32,14,14,1]{0,3,2,1:T(2,128)(2,1)S(1)}, bf16[32,14,14,1]{0,3,2,1:T(2,128)(2,1)S(1)}, u32[]{:S(2)}, u32[]{:S(2)}) %collective-permute-start.15) | collective-permute-done | bytes 12576 | tf_op jit(solution)/shard_map/ppermute | solution.py:32
  137.9 7.0 %fusion.91 = (f32[1,32,12,12,12]{1,0,4,3,2:T(1,128)}, bf16[1,32,12,12,12]{1,0,4,3,2:T(2,128)(2,1)S(1)}) fusion(bf16[32,32,3,3,3]{0,4,3,2,1:T(4,128)(2,1)S(1)} %reshape.107, bf16[1,32,14,14,14]{1,4,3,2,0:T(8,128)(2,1)S(1)} %maximum_bitcast_fusion.1), kind=kOutput, calls=%fused_computation.180 | convolution fusion | flops 95717376 | bytes 562688 | tf_op jit(solution)/shard_map/conv_general_dilated | solution.py:37
  161.8 7.8 %collective-permute-done.19 = bf16[64,8,1,6]{0,3,2,1:T(8,128)(2,1)S(1)} collective-permute-done((bf16[64,8,1,6]{0,3,2,1:T(8,128)(2,1)S(1)}, bf16[64,8,1,6]{0,3,2,1:T(8,128)(2,1)S(1)}, u32[]{:S(2)}, u32[]{:S(2)}) %collective-permute-start.19) | collective-permute-done | bytes 6176 | tf_op jit(solution)/shard_map/ppermute | solution.py:32
  171.8 9.5 %collective-permute-start.21 = (bf16[64,8,8,1]{0,3,2,1:T(2,128)(2,1)S(1)}, bf16[64,8,8,1]{0,3,2,1:T(2,128)(2,1)S(1)}, u32[]{:S(2)}, u32[]{:S(2)}) collective-permute-start(bf16[64,8,8,1]{0,3,2,1:T(2,128)(2,1)S(1)} %get-tuple-element.35), channel_id=1, source_target_pairs={{63,0},{0,1},{1,2},{2,3},{3,4},{4,5},{5,6},{6,7},{7,8},{8,9},{9,10... | collective-permute-start | bytes 24584 | tf_op jit(solution)/shard_map/ppermute | solution.py:32
  189.8 10.4 %collective-permute-done.23 = bf16[64,8,8,1]{0,3,2,1:T(2,128)(2,1)S(1)} collective-permute-done((bf16[64,8,8,1]{0,3,2,1:T(2,128)(2,1)S(1)}, bf16[64,8,8,1]{0,3,2,1:T(2,128)(2,1)S(1)}, u32[]{:S(2)}, u32[]{:S(2)}) %collective-permute-start.23) | collective-permute-done | bytes 8224 | tf_op jit(solution)/shard_map/ppermute | solution.py:32
  217.2 7.7 %collective-permute-done.27 = bf16[64,8,1,6]{0,3,2,1:T(8,128)(2,1)S(1)} collective-permute-done((bf16[64,8,1,6]{0,3,2,1:T(8,128)(2,1)S(1)}, bf16[64,8,1,6]{0,3,2,1:T(8,128)(2,1)S(1)}, u32[]{:S(2)}, u32[]{:S(2)}) %collective-permute-start.27) | collective-permute-done | bytes 6176 | tf_op jit(solution)/shard_map/ppermute | solution.py:32
  227.6 8.3 %collective-permute-start.29 = (bf16[64,8,8,1]{0,3,2,1:T(2,128)(2,1)S(1)}, bf16[64,8,8,1]{0,3,2,1:T(2,128)(2,1)S(1)}, u32[]{:S(2)}, u32[]{:S(2)}) collective-permute-start(bf16[64,8,8,1]{0,3,2,1:T(2,128)(2,1)S(1)} %get-tuple-element.33), channel_id=1, source_target_pairs={{63,0},{0,1},{1,2},{2,3},{3,4},{4,5},{5,6},{6,7},{7,8},{8,9},{9,10... | collective-permute-start | bytes 24584 | tf_op jit(solution)/shard_map/ppermute | solution.py:32
  245.6 10.2 %collective-permute-done.31 = bf16[64,8,8,1]{0,3,2,1:T(2,128)(2,1)S(1)} collective-permute-done((bf16[64,8,8,1]{0,3,2,1:T(2,128)(2,1)S(1)}, bf16[64,8,8,1]{0,3,2,1:T(2,128)(2,1)S(1)}, u32[]{:S(2)}, u32[]{:S(2)}) %collective-permute-start.31) | collective-permute-done | bytes 8224 | tf_op jit(solution)/shard_map/ppermute | solution.py:32
  273.6 7.8 %collective-permute-done.35 = bf16[256,5,1,3]{0,3,2,1:T(4,128)(2,1)S(1)} collective-permute-done((bf16[256,5,1,3]{0,3,2,1:T(4,128)(2,1)S(1)}, bf16[256,5,1,3]{0,3,2,1:T(4,128)(2,1)S(1)}, u32[]{:S(2)}, u32[]{:S(2)}) %collective-permute-start.35) | collective-permute-done | bytes 7712 | tf_op jit(solution)/shard_map/ppermute | solution.py:32
  301.1 10.1 %collective-permute-done.39 = bf16[256,5,5,1]{0,3,2,1:T(2,128)(2,1)S(1)} collective-permute-done((bf16[256,5,5,1]{0,3,2,1:T(2,128)(2,1)S(1)}, bf16[256,5,5,1]{0,3,2,1:T(2,128)(2,1)S(1)}, u32[]{:S(2)}, u32[]{:S(2)}) %collective-permute-start.39) | collective-permute-done | bytes 12832 | tf_op jit(solution)/shard_map/ppermute | solution.py:32
  317.4 8.9 %reshape_reshape.6 = bf16[256,256,3,3,3]{0,4,3,2,1:T(4,128)(2,1)} reshape(bf16[256,4,1728]{0,2,1:T(8,128)(2,1)} %bitcast.103) | data formatting | bytes 7077888 | tf_op jit(solution)/shard_map/reshape;reshape | solution.py:36
  345.0 7.6 %collective-permute-done.43 = bf16[256,5,1,3]{0,3,2,1:T(4,128)(2,1)S(1)} collective-permute-done((bf16[256,5,1,3]{0,3,2,1:T(4,128)(2,1)S(1)}, bf16[256,5,1,3]{0,3,2,1:T(4,128)(2,1)S(1)}, u32[]{:S(2)}, u32[]{:S(2)}) %collective-permute-start.43) | collective-permute-done | bytes 7712 | tf_op jit(solution)/shard_map/ppermute | solution.py:32
  368.1 8.9 %reshape_reshape.7 = bf16[256,256,3,3,3]{0,4,3,2,1:T(4,128)(2,1)} reshape(bf16[256,4,1728]{0,2,1:T(8,128)(2,1)} %bitcast.104) | data formatting | bytes 7077888 | tf_op jit(solution)/shard_map/reshape;reshape | solution.py:36
  387.2 9.8 %collective-permute-done.47 = bf16[256,5,5,1]{0,3,2,1:T(2,128)(2,1)S(1)} collective-permute-done((bf16[256,5,5,1]{0,3,2,1:T(2,128)(2,1)S(1)}, bf16[256,5,5,1]{0,3,2,1:T(2,128)(2,1)S(1)}, u32[]{:S(2)}, u32[]{:S(2)}) %collective-permute-start.47) | collective-permute-done | bytes 12832 | tf_op jit(solution)/shard_map/ppermute | solution.py:32
  422.9 7.7 %collective-permute-done.51 = bf16[64,8,1,6]{0,3,2,1:T(8,128)(2,1)S(1)} collective-permute-done((bf16[64,8,1,6]{0,3,2,1:T(8,128)(2,1)S(1)}, bf16[64,8,1,6]{0,3,2,1:T(8,128)(2,1)S(1)}, u32[]{:S(2)}, u32[]{:S(2)}) %collective-permute-start.51) | collective-permute-done | bytes 6176 | tf_op jit(solution)/shard_map/ppermute | solution.py:32
  451.8 9.9 %collective-permute-done.55 = bf16[64,8,8,1]{0,3,2,1:T(2,128)(2,1)S(1)} collective-permute-done((bf16[64,8,8,1]{0,3,2,1:T(2,128)(2,1)S(1)}, bf16[64,8,8,1]{0,3,2,1:T(2,128)(2,1)S(1)}, u32[]{:S(2)}, u32[]{:S(2)}) %collective-permute-start.55) | collective-permute-done | bytes 8224 | tf_op jit(solution)/shard_map/ppermute | solution.py:32
  478.6 7.7 %collective-permute-done.59 = bf16[64,8,1,6]{0,3,2,1:T(8,128)(2,1)S(1)} collective-permute-done((bf16[64,8,1,6]{0,3,2,1:T(8,128)(2,1)S(1)}, bf16[64,8,1,6]{0,3,2,1:T(8,128)(2,1)S(1)}, u32[]{:S(2)}, u32[]{:S(2)}) %collective-permute-start.59) | collective-permute-done | bytes 6176 | tf_op jit(solution)/shard_map/ppermute | solution.py:32
  489.4 7.0 %collective-permute-start.61 = (bf16[64,8,8,1]{0,3,2,1:T(2,128)(2,1)S(1)}, bf16[64,8,8,1]{0,3,2,1:T(2,128)(2,1)S(1)}, u32[]{:S(2)}, u32[]{:S(2)}) collective-permute-start(bf16[64,8,8,1]{0,3,2,1:T(2,128)(2,1)S(1)} %get-tuple-element.29), channel_id=1, source_target_pairs={{63,0},{0,1},{1,2},{2,3},{3,4},{4,5},{5,6},{6,7},{7,8},{8,9},{9,10... | collective-permute-start | bytes 24584 | tf_op jit(solution)/shard_map/ppermute | solution.py:32
  506.8 9.7 %collective-permute-done.63 = bf16[64,8,8,1]{0,3,2,1:T(2,128)(2,1)S(1)} collective-permute-done((bf16[64,8,8,1]{0,3,2,1:T(2,128)(2,1)S(1)}, bf16[64,8,8,1]{0,3,2,1:T(2,128)(2,1)S(1)}, u32[]{:S(2)}, u32[]{:S(2)}) %collective-permute-start.63) | collective-permute-done | bytes 8224 | tf_op jit(solution)/shard_map/ppermute | solution.py:32
  545.6 8.1 %collective-permute-done.67 = bf16[32,14,1,12]{0,3,2,1:T(8,128)(2,1)S(1)} collective-permute-done((bf16[32,14,1,12]{0,3,2,1:T(8,128)(2,1)S(1)}, bf16[32,14,1,12]{0,3,2,1:T(8,128)(2,1)S(1)}, u32[]{:S(2)}, u32[]{:S(2)}) %collective-permute-start.67) | collective-permute-done | bytes 10784 | tf_op jit(solution)/shard_map/ppermute | solution.py:32
  556.8 7.1 %collective-permute-start.69 = (bf16[32,14,14,1]{0,3,2,1:T(2,128)(2,1)S(1)}, bf16[32,14,14,1]{0,3,2,1:T(2,128)(2,1)S(1)}, u32[]{:S(2)}, u32[]{:S(2)}) collective-permute-start(bf16[32,14,14,1]{0,3,2,1:T(2,128)(2,1)S(1)} %get-tuple-element.7), channel_id=1, source_target_pairs={{63,0},{0,1},{1,2},{2,3},{3,4},{4,5},{5,6},{6,7},{7,8},{8,9},{9,10... | collective-permute-start | bytes 37640 | tf_op jit(solution)/shard_map/ppermute | solution.py:32
  574.0 10.5 %collective-permute-done.71 = bf16[32,14,14,1]{0,3,2,1:T(2,128)(2,1)S(1)} collective-permute-done((bf16[32,14,14,1]{0,3,2,1:T(2,128)(2,1)S(1)}, bf16[32,14,14,1]{0,3,2,1:T(2,128)(2,1)S(1)}, u32[]{:S(2)}, u32[]{:S(2)}) %collective-permute-start.71) | collective-permute-done | bytes 12576 | tf_op jit(solution)/shard_map/ppermute | solution.py:32
  607.5 8.1 %collective-permute-done.75 = bf16[32,14,1,12]{0,3,2,1:T(8,128)(2,1)S(1)} collective-permute-done((bf16[32,14,1,12]{0,3,2,1:T(8,128)(2,1)S(1)}, bf16[32,14,1,12]{0,3,2,1:T(8,128)(2,1)S(1)}, u32[]{:S(2)}, u32[]{:S(2)}) %collective-permute-start.75) | collective-permute-done | bytes 10784 | tf_op jit(solution)/shard_map/ppermute | solution.py:32
  636.2 10.5 %collective-permute-done.79 = bf16[32,14,14,1]{0,3,2,1:T(2,128)(2,1)S(1)} collective-permute-done((bf16[32,14,14,1]{0,3,2,1:T(2,128)(2,1)S(1)}, bf16[32,14,14,1]{0,3,2,1:T(2,128)(2,1)S(1)}, u32[]{:S(2)}, u32[]{:S(2)}) %collective-permute-start.79) | collective-permute-done | bytes 12576 | tf_op jit(solution)/shard_map/ppermute | solution.py:32
  647.5 7.8 %fusion.57 = bf16[32,12,12,12]{0,3,2,1:T(8,128)(2,1)S(1)} fusion(bf16[1,32,14,14,14]{1,4,3,2,0:T(8,128)(2,1)S(1)} %maximum_bitcast_fusion.3, bf16[32,32,3,3,3]{0,4,3,2,1:T(4,128)(2,1)S(1)} %reshape.121), kind=kOutput, calls=%fused_computation.40 | convolution fusion | flops 95662080 | bytes 341504 | tf_op jit(solution)/shard_map/conv_general_dilated | solution.py:37
  (281 shorter events, 364.2 us)
Async XLA Ops:
  6.5 304.9 %all-gather.3.cloned.1.call-start = ((), (), s32[]{:S(2)}) async-start(), calls=%async_computation | async-start | bytes 3727360 | tf_op jit(solution)/shard_map/all_gather | solution.py:119
  7.3 354.9 %all-gather.5.cloned.1.call-start = ((), (), s32[]{:S(2)}) async-start(), calls=%async_computation.1 | async-start | bytes 3727360 | tf_op jit(solution)/shard_map/all_gather | solution.py:119
  42.6 19.9 %collective-permute-start.4 = (bf16[32,14,14,1]{0,3,2,1:T(2,128)(2,1)S(1)}, bf16[32,14,14,1]{0,3,2,1:T(2,128)(2,1)S(1)}, u32[]{:S(2)}, u32[]{:S(2)}) collective-permute-start(bf16[32,14,14,1]{0,3,2,1:T(2,128)(2,1)S(1)} %get-tuple-element.11), channel_id=1, source_target_pairs={{7,0},{8,1},{9,2},{10,3},{11,4},{12,5},{13,6},{14,7},{15,8},{16,9}... | collective-permute-start | bytes 37640 | tf_op jit(solution)/shard_map/ppermute | solution.py:32
  45.4 17.2 %collective-permute-start.5 = (bf16[32,14,14,1]{0,3,2,1:T(2,128)(2,1)S(1)}, bf16[32,14,14,1]{0,3,2,1:T(2,128)(2,1)S(1)}, u32[]{:S(2)}, u32[]{:S(2)}) collective-permute-start(bf16[32,14,14,1]{0,3,2,1:T(2,128)(2,1)S(1)} %get-tuple-element.11), channel_id=1, source_target_pairs={{63,0},{0,1},{1,2},{2,3},{3,4},{4,5},{5,6},{6,7},{7,8},{8,9},{9,10... | collective-permute-start | bytes 37640 | tf_op jit(solution)/shard_map/ppermute | solution.py:32
  58.6 15.4 %collective-permute-start.7 = (bf16[32,14,14,1]{0,3,2,1:T(2,128)(2,1)S(1)}, bf16[32,14,14,1]{0,3,2,1:T(2,128)(2,1)S(1)}, u32[]{:S(2)}, u32[]{:S(2)}) collective-permute-start(bf16[32,14,14,1]{0,3,2,1:T(2,128)(2,1)S(1)} %get-tuple-element.12), channel_id=1, source_target_pairs={{1,0},{2,1},{3,2},{4,3},{5,4},{6,5},{7,6},{8,7},{9,8},{10,9},{11,1... | collective-permute-start | bytes 37640 | tf_op jit(solution)/shard_map/ppermute | solution.py:32
  105.3 20.5 %collective-permute-start.12 = (bf16[32,14,14,1]{0,3,2,1:T(2,128)(2,1)S(1)}, bf16[32,14,14,1]{0,3,2,1:T(2,128)(2,1)S(1)}, u32[]{:S(2)}, u32[]{:S(2)}) collective-permute-start(bf16[32,14,14,1]{0,3,2,1:T(2,128)(2,1)S(1)} %get-tuple-element.9), channel_id=1, source_target_pairs={{7,0},{8,1},{9,2},{10,3},{11,4},{12,5},{13,6},{14,7},{15,8},{16,9}... | collective-permute-start | bytes 37640 | tf_op jit(solution)/shard_map/ppermute | solution.py:32
  107.6 18.1 %collective-permute-start.13 = (bf16[32,14,14,1]{0,3,2,1:T(2,128)(2,1)S(1)}, bf16[32,14,14,1]{0,3,2,1:T(2,128)(2,1)S(1)}, u32[]{:S(2)}, u32[]{:S(2)}) collective-permute-start(bf16[32,14,14,1]{0,3,2,1:T(2,128)(2,1)S(1)} %get-tuple-element.9), channel_id=1, source_target_pairs={{63,0},{0,1},{1,2},{2,3},{3,4},{4,5},{5,6},{6,7},{7,8},{8,9},{9,10... | collective-permute-start | bytes 37640 | tf_op jit(solution)/shard_map/ppermute | solution.py:32
  121.3 15.8 %collective-permute-start.15 = (bf16[32,14,14,1]{0,3,2,1:T(2,128)(2,1)S(1)}, bf16[32,14,14,1]{0,3,2,1:T(2,128)(2,1)S(1)}, u32[]{:S(2)}, u32[]{:S(2)}) collective-permute-start(bf16[32,14,14,1]{0,3,2,1:T(2,128)(2,1)S(1)} %get-tuple-element.10), channel_id=1, source_target_pairs={{1,0},{2,1},{3,2},{4,3},{5,4},{6,5},{7,6},{8,7},{9,8},{10,9},{11,1... | collective-permute-start | bytes 37640 | tf_op jit(solution)/shard_map/ppermute | solution.py:32
  169.6 20.1 %collective-permute-start.20 = (bf16[64,8,8,1]{0,3,2,1:T(2,128)(2,1)S(1)}, bf16[64,8,8,1]{0,3,2,1:T(2,128)(2,1)S(1)}, u32[]{:S(2)}, u32[]{:S(2)}) collective-permute-start(bf16[64,8,8,1]{0,3,2,1:T(2,128)(2,1)S(1)} %get-tuple-element.35), channel_id=1, source_target_pairs={{7,0},{8,1},{9,2},{10,3},{11,4},{12,5},{13,6},{14,7},{15,8},{16,9}... | collective-permute-start | bytes 24584 | tf_op jit(solution)/shard_map/ppermute | solution.py:32
  171.8 17.9 %collective-permute-start.21 = (bf16[64,8,8,1]{0,3,2,1:T(2,128)(2,1)S(1)}, bf16[64,8,8,1]{0,3,2,1:T(2,128)(2,1)S(1)}, u32[]{:S(2)}, u32[]{:S(2)}) collective-permute-start(bf16[64,8,8,1]{0,3,2,1:T(2,128)(2,1)S(1)} %get-tuple-element.35), channel_id=1, source_target_pairs={{63,0},{0,1},{1,2},{2,3},{3,4},{4,5},{5,6},{6,7},{7,8},{8,9},{9,10... | collective-permute-start | bytes 24584 | tf_op jit(solution)/shard_map/ppermute | solution.py:32
  185.8 14.4 %collective-permute-start.23 = (bf16[64,8,8,1]{0,3,2,1:T(2,128)(2,1)S(1)}, bf16[64,8,8,1]{0,3,2,1:T(2,128)(2,1)S(1)}, u32[]{:S(2)}, u32[]{:S(2)}) collective-permute-start(bf16[64,8,8,1]{0,3,2,1:T(2,128)(2,1)S(1)} %get-tuple-element.36), channel_id=1, source_target_pairs={{1,0},{2,1},{3,2},{4,3},{5,4},{6,5},{7,6},{8,7},{9,8},{10,9},{11,1... | collective-permute-start | bytes 24584 | tf_op jit(solution)/shard_map/ppermute | solution.py:32
  225.0 20.5 %collective-permute-start.28 = (bf16[64,8,8,1]{0,3,2,1:T(2,128)(2,1)S(1)}, bf16[64,8,8,1]{0,3,2,1:T(2,128)(2,1)S(1)}, u32[]{:S(2)}, u32[]{:S(2)}) collective-permute-start(bf16[64,8,8,1]{0,3,2,1:T(2,128)(2,1)S(1)} %get-tuple-element.33), channel_id=1, source_target_pairs={{7,0},{8,1},{9,2},{10,3},{11,4},{12,5},{13,6},{14,7},{15,8},{16,9}... | collective-permute-start | bytes 24584 | tf_op jit(solution)/shard_map/ppermute | solution.py:32
  227.6 17.9 %collective-permute-start.29 = (bf16[64,8,8,1]{0,3,2,1:T(2,128)(2,1)S(1)}, bf16[64,8,8,1]{0,3,2,1:T(2,128)(2,1)S(1)}, u32[]{:S(2)}, u32[]{:S(2)}) collective-permute-start(bf16[64,8,8,1]{0,3,2,1:T(2,128)(2,1)S(1)} %get-tuple-element.33), channel_id=1, source_target_pairs={{63,0},{0,1},{1,2},{2,3},{3,4},{4,5},{5,6},{6,7},{7,8},{8,9},{9,10... | collective-permute-start | bytes 24584 | tf_op jit(solution)/shard_map/ppermute | solution.py:32
  241.4 14.4 %collective-permute-start.31 = (bf16[64,8,8,1]{0,3,2,1:T(2,128)(2,1)S(1)}, bf16[64,8,8,1]{0,3,2,1:T(2,128)(2,1)S(1)}, u32[]{:S(2)}, u32[]{:S(2)}) collective-permute-start(bf16[64,8,8,1]{0,3,2,1:T(2,128)(2,1)S(1)} %get-tuple-element.34), channel_id=1, source_target_pairs={{1,0},{2,1},{3,2},{4,3},{5,4},{6,5},{7,6},{8,7},{9,8},{10,9},{11,1... | collective-permute-start | bytes 24584 | tf_op jit(solution)/shard_map/ppermute | solution.py:32
  281.5 19.5 %collective-permute-start.36 = (bf16[256,5,5,1]{0,3,2,1:T(2,128)(2,1)S(1)}, bf16[256,5,5,1]{0,3,2,1:T(2,128)(2,1)S(1)}, u32[]{:S(2)}, u32[]{:S(2)}) collective-permute-start(bf16[256,5,5,1]{0,3,2,1:T(2,128)(2,1)S(1)} %get-tuple-element.55), channel_id=1, source_target_pairs={{7,0},{8,1},{9,2},{10,3},{11,4},{12,5},{13,6},{14,7},{15,8},{16,9}... | collective-permute-start | bytes 38408 | tf_op jit(solution)/shard_map/ppermute | solution.py:32
  284.4 16.6 %collective-permute-start.37 = (bf16[256,5,5,1]{0,3,2,1:T(2,128)(2,1)S(1)}, bf16[256,5,5,1]{0,3,2,1:T(2,128)(2,1)S(1)}, u32[]{:S(2)}, u32[]{:S(2)}) collective-permute-start(bf16[256,5,5,1]{0,3,2,1:T(2,128)(2,1)S(1)} %get-tuple-element.55), channel_id=1, source_target_pairs={{63,0},{0,1},{1,2},{2,3},{3,4},{4,5},{5,6},{6,7},{7,8},{8,9},{9,10... | collective-permute-start | bytes 38408 | tf_op jit(solution)/shard_map/ppermute | solution.py:32
  297.1 14.2 %collective-permute-start.39 = (bf16[256,5,5,1]{0,3,2,1:T(2,128)(2,1)S(1)}, bf16[256,5,5,1]{0,3,2,1:T(2,128)(2,1)S(1)}, u32[]{:S(2)}, u32[]{:S(2)}) collective-permute-start(bf16[256,5,5,1]{0,3,2,1:T(2,128)(2,1)S(1)} %get-tuple-element.56), channel_id=1, source_target_pairs={{1,0},{2,1},{3,2},{4,3},{5,4},{6,5},{7,6},{8,7},{9,8},{10,9},{11,1... | collective-permute-start | bytes 38408 | tf_op jit(solution)/shard_map/ppermute | solution.py:32
  352.8 34.4 %collective-permute-start.44 = (bf16[256,5,5,1]{0,3,2,1:T(2,128)(2,1)S(1)}, bf16[256,5,5,1]{0,3,2,1:T(2,128)(2,1)S(1)}, u32[]{:S(2)}, u32[]{:S(2)}) collective-permute-start(bf16[256,5,5,1]{0,3,2,1:T(2,128)(2,1)S(1)} %get-tuple-element.53), channel_id=1, source_target_pairs={{7,0},{8,1},{9,2},{10,3},{11,4},{12,5},{13,6},{14,7},{15,8},{16,9}... | collective-permute-start | bytes 38408 | tf_op jit(solution)/shard_map/ppermute | solution.py:32
  355.6 31.6 %collective-permute-start.45 = (bf16[256,5,5,1]{0,3,2,1:T(2,128)(2,1)S(1)}, bf16[256,5,5,1]{0,3,2,1:T(2,128)(2,1)S(1)}, u32[]{:S(2)}, u32[]{:S(2)}) collective-permute-start(bf16[256,5,5,1]{0,3,2,1:T(2,128)(2,1)S(1)} %get-tuple-element.53), channel_id=1, source_target_pairs={{63,0},{0,1},{1,2},{2,3},{3,4},{4,5},{5,6},{6,7},{7,8},{8,9},{9,10... | collective-permute-start | bytes 38408 | tf_op jit(solution)/shard_map/ppermute | solution.py:32
  383.2 13.9 %collective-permute-start.47 = (bf16[256,5,5,1]{0,3,2,1:T(2,128)(2,1)S(1)}, bf16[256,5,5,1]{0,3,2,1:T(2,128)(2,1)S(1)}, u32[]{:S(2)}, u32[]{:S(2)}) collective-permute-start(bf16[256,5,5,1]{0,3,2,1:T(2,128)(2,1)S(1)} %get-tuple-element.54), channel_id=1, source_target_pairs={{1,0},{2,1},{3,2},{4,3},{5,4},{6,5},{7,6},{8,7},{9,8},{10,9},{11,1... | collective-permute-start | bytes 38408 | tf_op jit(solution)/shard_map/ppermute | solution.py:32
  430.7 21.0 %collective-permute-start.52 = (bf16[64,8,8,1]{0,3,2,1:T(2,128)(2,1)S(1)}, bf16[64,8,8,1]{0,3,2,1:T(2,128)(2,1)S(1)}, u32[]{:S(2)}, u32[]{:S(2)}) collective-permute-start(bf16[64,8,8,1]{0,3,2,1:T(2,128)(2,1)S(1)} %get-tuple-element.31), channel_id=1, source_target_pairs={{7,0},{8,1},{9,2},{10,3},{11,4},{12,5},{13,6},{14,7},{15,8},{16,9}... | collective-permute-start | bytes 24584 | tf_op jit(solution)/shard_map/ppermute | solution.py:32
  433.8 17.9 %collective-permute-start.53 = (bf16[64,8,8,1]{0,3,2,1:T(2,128)(2,1)S(1)}, bf16[64,8,8,1]{0,3,2,1:T(2,128)(2,1)S(1)}, u32[]{:S(2)}, u32[]{:S(2)}) collective-permute-start(bf16[64,8,8,1]{0,3,2,1:T(2,128)(2,1)S(1)} %get-tuple-element.31), channel_id=1, source_target_pairs={{63,0},{0,1},{1,2},{2,3},{3,4},{4,5},{5,6},{6,7},{7,8},{8,9},{9,10... | collective-permute-start | bytes 24584 | tf_op jit(solution)/shard_map/ppermute | solution.py:32
  447.8 13.9 %collective-permute-start.55 = (bf16[64,8,8,1]{0,3,2,1:T(2,128)(2,1)S(1)}, bf16[64,8,8,1]{0,3,2,1:T(2,128)(2,1)S(1)}, u32[]{:S(2)}, u32[]{:S(2)}) collective-permute-start(bf16[64,8,8,1]{0,3,2,1:T(2,128)(2,1)S(1)} %get-tuple-element.32), channel_id=1, source_target_pairs={{1,0},{2,1},{3,2},{4,3},{5,4},{6,5},{7,6},{8,7},{9,8},{10,9},{11,1... | collective-permute-start | bytes 24584 | tf_op jit(solution)/shard_map/ppermute | solution.py:32
  486.4 20.3 %collective-permute-start.60 = (bf16[64,8,8,1]{0,3,2,1:T(2,128)(2,1)S(1)}, bf16[64,8,8,1]{0,3,2,1:T(2,128)(2,1)S(1)}, u32[]{:S(2)}, u32[]{:S(2)}) collective-permute-start(bf16[64,8,8,1]{0,3,2,1:T(2,128)(2,1)S(1)} %get-tuple-element.29), channel_id=1, source_target_pairs={{7,0},{8,1},{9,2},{10,3},{11,4},{12,5},{13,6},{14,7},{15,8},{16,9}... | collective-permute-start | bytes 24584 | tf_op jit(solution)/shard_map/ppermute | solution.py:32
  489.4 17.2 %collective-permute-start.61 = (bf16[64,8,8,1]{0,3,2,1:T(2,128)(2,1)S(1)}, bf16[64,8,8,1]{0,3,2,1:T(2,128)(2,1)S(1)}, u32[]{:S(2)}, u32[]{:S(2)}) collective-permute-start(bf16[64,8,8,1]{0,3,2,1:T(2,128)(2,1)S(1)} %get-tuple-element.29), channel_id=1, source_target_pairs={{63,0},{0,1},{1,2},{2,3},{3,4},{4,5},{5,6},{6,7},{7,8},{8,9},{9,10... | collective-permute-start | bytes 24584 | tf_op jit(solution)/shard_map/ppermute | solution.py:32
  502.5 13.9 %collective-permute-start.63 = (bf16[64,8,8,1]{0,3,2,1:T(2,128)(2,1)S(1)}, bf16[64,8,8,1]{0,3,2,1:T(2,128)(2,1)S(1)}, u32[]{:S(2)}, u32[]{:S(2)}) collective-permute-start(bf16[64,8,8,1]{0,3,2,1:T(2,128)(2,1)S(1)} %get-tuple-element.30), channel_id=1, source_target_pairs={{1,0},{2,1},{3,2},{4,3},{5,4},{6,5},{7,6},{8,7},{9,8},{10,9},{11,1... | collective-permute-start | bytes 24584 | tf_op jit(solution)/shard_map/ppermute | solution.py:32
  554.0 19.9 %collective-permute-start.68 = (bf16[32,14,14,1]{0,3,2,1:T(2,128)(2,1)S(1)}, bf16[32,14,14,1]{0,3,2,1:T(2,128)(2,1)S(1)}, u32[]{:S(2)}, u32[]{:S(2)}) collective-permute-start(bf16[32,14,14,1]{0,3,2,1:T(2,128)(2,1)S(1)} %get-tuple-element.7), channel_id=1, source_target_pairs={{7,0},{8,1},{9,2},{10,3},{11,4},{12,5},{13,6},{14,7},{15,8},{16,9}... | collective-permute-start | bytes 37640 | tf_op jit(solution)/shard_map/ppermute | solution.py:32
  556.8 17.0 %collective-permute-start.69 = (bf16[32,14,14,1]{0,3,2,1:T(2,128)(2,1)S(1)}, bf16[32,14,14,1]{0,3,2,1:T(2,128)(2,1)S(1)}, u32[]{:S(2)}, u32[]{:S(2)}) collective-permute-start(bf16[32,14,14,1]{0,3,2,1:T(2,128)(2,1)S(1)} %get-tuple-element.7), channel_id=1, source_target_pairs={{63,0},{0,1},{1,2},{2,3},{3,4},{4,5},{5,6},{6,7},{7,8},{8,9},{9,10... | collective-permute-start | bytes 37640 | tf_op jit(solution)/shard_map/ppermute | solution.py:32
  569.9 14.7 %collective-permute-start.71 = (bf16[32,14,14,1]{0,3,2,1:T(2,128)(2,1)S(1)}, bf16[32,14,14,1]{0,3,2,1:T(2,128)(2,1)S(1)}, u32[]{:S(2)}, u32[]{:S(2)}) collective-permute-start(bf16[32,14,14,1]{0,3,2,1:T(2,128)(2,1)S(1)} %get-tuple-element.8), channel_id=1, source_target_pairs={{1,0},{2,1},{3,2},{4,3},{5,4},{6,5},{7,6},{8,7},{9,8},{10,9},{11,1... | collective-permute-start | bytes 37640 | tf_op jit(solution)/shard_map/ppermute | solution.py:32
  615.8 20.1 %collective-permute-start.76 = (bf16[32,14,14,1]{0,3,2,1:T(2,128)(2,1)S(1)}, bf16[32,14,14,1]{0,3,2,1:T(2,128)(2,1)S(1)}, u32[]{:S(2)}, u32[]{:S(2)}) collective-permute-start(bf16[32,14,14,1]{0,3,2,1:T(2,128)(2,1)S(1)} %get-tuple-element.5), channel_id=1, source_target_pairs={{7,0},{8,1},{9,2},{10,3},{11,4},{12,5},{13,6},{14,7},{15,8},{16,9}... | collective-permute-start | bytes 37640 | tf_op jit(solution)/shard_map/ppermute | solution.py:32
  619.0 17.0 %collective-permute-start.77 = (bf16[32,14,14,1]{0,3,2,1:T(2,128)(2,1)S(1)}, bf16[32,14,14,1]{0,3,2,1:T(2,128)(2,1)S(1)}, u32[]{:S(2)}, u32[]{:S(2)}) collective-permute-start(bf16[32,14,14,1]{0,3,2,1:T(2,128)(2,1)S(1)} %get-tuple-element.5), channel_id=1, source_target_pairs={{63,0},{0,1},{1,2},{2,3},{3,4},{4,5},{5,6},{6,7},{7,8},{8,9},{9,10... | collective-permute-start | bytes 37640 | tf_op jit(solution)/shard_map/ppermute | solution.py:32
  632.0 14.7 %collective-permute-start.79 = (bf16[32,14,14,1]{0,3,2,1:T(2,128)(2,1)S(1)}, bf16[32,14,14,1]{0,3,2,1:T(2,128)(2,1)S(1)}, u32[]{:S(2)}, u32[]{:S(2)}) collective-permute-start(bf16[32,14,14,1]{0,3,2,1:T(2,128)(2,1)S(1)} %get-tuple-element.6), channel_id=1, source_target_pairs={{1,0},{2,1},{3,2},{4,3},{5,4},{6,5},{7,6},{8,7},{9,8},{10,9},{11,1... | collective-permute-start | bytes 37640 | tf_op jit(solution)/shard_map/ppermute | solution.py:32
  (61 other events, 1188.9 us)
Sparse Core Ops, SparseCore 0:
  11.8 164.6 all-gather.2
  181.1 147.2 all-gather.4
where the time goes:
time: 674 us; the launch traced here: 664 us
  starting transfers between devices  344 us (51%)
  waiting for transfers between devices  202 us (30%)
  local copies, waits for them, and re-layouts  53.1 us (8%)
  matrix products  40.3 us (6%)
  between operations  15.6 us (2%)
  other arithmetic  8.97 us (1%)
    ppermute x60, starting transfers between devices, from_behind(): return lax.ppermute(block, axis, route)  268 us
    ppermute x60, waiting for transfers between devices, from_behind(): return lax.ppermute(block, axis, route)  187 us
    ppermute x10, starting transfers between devices, with_halo(): lax.ppermute(head, axis, [((i + 1) % count, i) for i in range(count)])  56.3 us
    conv_general_dilated x10, matrix products, conv_taps(): lax.conv_general_dilated(padded[None], kernel, (1, 1, 1), 'VALID', dimens...  38.3 us
    ppermute x10, starting transfers between devices, with_halo(): lax.ppermute(tail, axis, [(i, (i + 1) % count) for i in range(count)])  19.3 us
    another operation x2, local copies, waits for them, and re-layouts, conv_taps(): kernel = weight.reshape(weight.shape[0], width_in, 3, 3, 3)  17.7 us
    ppermute x10, waiting for transfers between devices, with_halo(): lax.ppermute(head, axis, [((i + 1) % count, i) for i in range(count)])  14.6 us
  transfers between devices with their start and end apart: 82, of which 37 were waited for; matrix products, arithmetic and copies ran while one was open for 9% of the time, Pallas kernels for 0%

commit v1 on v0

v1 whole, which is shorter than its diff:
```python
import math

import jax
import jax.numpy as jnp
import numpy as np
from jax import lax
from jax.experimental import pallas as pl
from jax.experimental.pallas import tpu as pltpu
from jax.sharding import PartitionSpec as P

MESH = pl.DeviceIdType.MESH
BF = jnp.bfloat16
F32 = jnp.float32
YZ8 = [(b, c) for b in (-1, 0, 1) for c in (-1, 0, 1) if (b, c) != (0, 0)]
ALL26 = [
    (a, b, c)
    for a in (-1, 0, 1)
    for b in (-1, 0, 1)
    for c in (-1, 0, 1)
    if (a, b, c) != (0, 0, 0)
]


class Level:
    def __init__(self, width, extent, stride, lanes, group):
        self.width, self.extent, self.stride, self.lanes = width, extent, stride, lanes
        self.planes = extent + 4
        self.share = lanes // 8
        self.per_tile = 128 // self.share
        self.tiles = -(-extent // self.per_tile)
        self.group = group

    def lane(self, y, z):
        return (y + 2) * self.stride + z + 2

    def region(self, step):
        e = self.extent
        return {-1: (0, 1), 0: tuple(range(e)), 1: (e - 2, e - 1)}[step]

    def tables(self):
        pack = np.zeros((self.lanes, self.lanes), np.float32)
        unpack = np.zeros((self.lanes, self.lanes), np.float32)
        for d, (b, c) in enumerate(YZ8):
            cell = 0
            for y in self.region(b):
                for z in self.region(c):
                    slot = d * self.share + cell
                    pack[self.lane(y, z), slot] = 1
                    unpack[slot, self.lane(y - self.extent * b, z - self.extent * c)] = 1
                    cell += 1
        return pack, unpack


FINE = Level(32, 12, 16, 256, 4)
MID = Level(64, 6, 10, 128, 5)
FLAT = 896
OUT1, OUT2 = 640, 384


def constants():
    place = np.zeros((144, 256), np.float32)
    for y in range(12):
        for z in range(12):
            place[y * 12 + z, FINE.lane(y, z)] = 1
    taps = np.zeros((864, 896), np.float32)
    for i in range(32):
        for t in range(27):
            taps[27 * i + t, 32 * t + i] = 1
    eight = np.zeros((256, 256), np.float32)
    for i in range(32):
        for t in range(8):
            eight[8 * i + t, 32 * t + i] = 1
    down = np.zeros((256, 128), np.float32)
    for y in range(6):
        for z in range(6):
            down[FINE.lane(2 * y, 2 * z), MID.lane(y, z)] = 1
    down_bottom = np.zeros((384, 128), np.float32)
    for j in range(3):
        for y in range(3):
            for z in range(3):
                down_bottom[128 * j + MID.lane(2 * y, 2 * z), 9 * j + 3 * y + z] = 1
    up_fine = np.zeros((128, 1024), np.float32)
    for y in range(16):
        for z in range(16):
            part = 2 * (y % 2) + z % 2
            up_fine[(y // 2 + 1) * 10 + z // 2 + 1, 256 * part + 16 * y + z] = 1
    up_mid = np.zeros((128, 512), np.float32)
    for y in range(10):
        for z in range(10):
            part = 2 * (y % 2) + z % 2
            up_mid[9 * (y // 2) + z // 2, 128 * part + 10 * y + z] = 1
    blocks = np.zeros((FLAT, FLAT), np.float32)
    for a in (-1, 0, 1):
        for b in (-1, 0, 1):
            for c in (-1, 0, 1):
                row = 32 * (9 * (a + 1) + 3 * (b + 1) + c + 1)
                for i in range(27):
                    x, y, z = i // 9 - 3 * a + 3, i // 3 % 3 - 3 * b + 3, i % 3 - 3 * c + 3
                    blocks[row + i, 81 * x + 9 * y + z] = 1
    pick = []
    for width in (32, 64):
        table = np.zeros((2 * width, 8 * width), np.float32)
        for a in range(2):
            for o in range(width):
                for part in range(4):
                    table[a * width + o, 8 * o + 4 * a + part] = 1
        pick.append(table)
    fine_pack, fine_unpack = FINE.tables()
    mid_pack, mid_unpack = MID.tables()
    return dict(
        place=place,
        leave=np.pad(place.T, ((0, 0), (0, 112))),
        taps=taps,
        eight=eight,
        down=down,
        down_bottom=down_bottom,
        up_fine=up_fine,
        up_mid=up_mid,
        blocks=blocks,
        pick_fine=pick[0],
        pick_mid=pick[1],
        fine_pack=fine_pack,
        fine_unpack=fine_unpack,
        mid_pack=mid_pack,
        mid_unpack=mid_unpack,
    )


NAMES = (
    "efa", "efb", "rf", "ema", "emb", "rm", "ba", "bb", "xm", "dma", "dmb", "xf", "dfa", "dfb",
)
CONST = tuple(constants().keys())


def ahead(value, shift):
    width = value.shape[1]
    shift = -shift % width
    return value if shift == 0 else pltpu.roll(value, shift, 1)


def dot(a, b):
    return jnp.dot(a, b, preferred_element_type=F32)


def dot_nt(a, b):
    return lax.dot_general(a, b, (((1,), (1,)), ((), ())), preferred_element_type=F32)


def group_of(rows, size):
    return lax.broadcasted_iota(jnp.int32, (rows, 128), 1) // size


def kernel(ngx, nyz, place_of, x_ref, *refs):
    w = dict(zip(NAMES, refs[: len(NAMES)]))
    refs = refs[len(NAMES) :]
    k = dict(zip(CONST, refs[: len(CONST)]))
    refs = refs[len(CONST) :]
    out_ref = refs[0]
    s = dict(zip(SCRATCH, refs[1:]))
    across = math.isqrt(nyz)
    nzh, ny, nx = place_of
    gx, yz = lax.axis_index("gx"), lax.axis_index("yz")

    def device(a, b, c):
        row, col = yz // across, yz % across
        return (
            (gx + a + ngx) % ngx,
            (row + b + across) % across * across + (col + c + across) % across,
        )

    zh, gy, gxx = yz // (ny * nx), yz // nx % ny, yz % nx
    core = gx % 2
    partner = (gx + 1 - 2 * core, yz)
    rs = 1024 // nyz

    def at(z, y, x):
        return z * ny * nx + y * nx + x

    z_peer = ((ngx // 2 - 1 - gx // 2) * 2 + core, at(1 - zh, gy, gxx))
    y_peers = [(gx, at(zh, (gy + d) % ny, gxx)) for d in range(1, ny)]
    x_next = (gx, at(zh, gy, (gxx + 1) % nx))
    x_last = (gx, at(zh, gy, (gxx + nx - 1) % nx))

    barrier = pltpu.get_barrier_semaphore()
    greet = [device(*d) for d in ALL26] + y_peers + [x_next, x_last, partner]
    if nzh == 2:
        greet.append(z_peer)
    for peer in greet:
        pl.semaphore_signal(barrier, inc=1, device_id=peer, device_id_type=MESH)

    started = []

    def send(src, dst, ssem, rsem, peer):
        copy = pltpu.make_async_remote_copy(
            src_ref=src, dst_ref=dst, send_sem=ssem, recv_sem=rsem, device_id=peer, device_id_type=MESH
        )
        copy.start()
        started.append(copy)
        return copy

    for level, ref in ((FINE, s["mid_f"]), (MID, s["mid_m"])):
        n, last = level.lanes, (level.planes - 1) * level.lanes
        ref[:, 0:n] = jnp.zeros((level.width, n), BF)
        ref[:, last : last + n] = jnp.zeros((level.width, n), BF)

    raw_x = s["raw_x"]
    planes = dot(x_ref[...], k["place"][...]).astype(BF)
    for p in range(12):
        raw_x[:, (p + 2) * 256 : (p + 3) * 256] = planes[32 * p : 32 * p + 32]

    def pack(level, raw, message):
        c, e, n = level.width, level.extent, level.lanes
        table = k["fine_pack" if level is FINE else "mid_pack"]
        which = group_of(c, level.share)
        for t in range(level.tiles):
            members = range(t * level.per_tile, min(e, (t + 1) * level.per_tile))
            rows = jnp.concatenate([raw[:, (p + 2) * n : (p + 3) * n] for p in members], axis=0)
            faces = dot(rows, table[...])
            for d in range(8):
                half, base = divmod(d * level.share, 128)
                tile = jnp.zeros((c, 128), F32)
                for q in range(len(members)):
                    part = faces[q * c : (q + 1) * c, 128 * half : 128 * half + 128]
                    tile = jnp.where(which == q, ahead(part, base - q * level.share), tile)
                message[d, t] = tile.astype(BF)

    def exchange(level, raw, message, arrived, ssem, rsem):
        n, e = level.lanes, level.extent
        copies = []
        for m, (a, b, c) in enumerate(ALL26):
            if (b, c) == (0, 0):
                src = raw.at[:, (e * n if a == 1 else 2 * n) : (e * n if a == 1 else 2 * n) + 2 * n]
                dst = raw.at[:, 0 : 2 * n] if a == 1 else raw.at[:, (e + 2) * n : (e + 4) * n]
            else:
                d = YZ8.index((b, c))
                if a == 0:
                    src, dst = message.at[d], arrived.at[1, d]
                else:
                    src = message.at[d, level.tiles - 1 if a == 1 else 0]
                    dst = arrived.at[2 if a == 1 else 0, d, 0]
            copies.append(send(src, dst, ssem.at[m], rsem.at[m], device(a, b, c)))
        return copies

    def unpack(level, raw, arrived, full, copies):
        c, e, n = level.width, level.extent, level.lanes
        table = k["fine_unpack" if level is FINE else "mid_unpack"]
        which = group_of(c, level.share)
        for copy in copies:
            copy.wait_recv()

        def halo(plane):
            p = plane - 2
            slot, tile = 1, p // level.per_tile
            if p < 0:
                slot, tile, p = 2, 0, p + e
            elif p >= e:
                slot, tile, p = 0, 0, p - e
            q = p % level.per_tile
            halves = []
            for half in range(n // 128):
                value = jnp.zeros((c, 128), F32)
                for d in range(8):
                    if d * level.share // 128 == half:
                        base = d * level.share % 128
                        piece = arrived[slot, d, tile].astype(F32)
                        value = jnp.where(
                            which == base // level.share, ahead(piece, q * level.share - base), value
                        )
                halves.append(value)
            return jnp.concatenate(halves, axis=1) if len(halves) > 1 else halves[0]

        step = 4 if level is FINE else 5
        for first in range(0, level.planes, step):
            members = range(first, first + step)
            rows = jnp.concatenate([halo(m) for m in members], axis=0).astype(BF)
            placed = dot(rows, table[...])
            for q, m in enumerate(members):
                own = raw[:, m * n : (m + 1) * n].astype(F32)
                full[:, m * n : (m + 1) * n] = (own + placed[q * c : (q + 1) * c]).astype(BF)

    def conv(level, src, weight, dst):
        c, n = level.width, level.lanes
        width = level.group * n
        cols, sums = (s["cols_f"], s["sums_f"]) if level is FINE else (s["cols_m"], s["sums_m"])

        def one(g, carry):
            lanes = pl.ds(pl.multiple_of(g * width, width), width)
            for ib in range(c // 32):
                rows = src[32 * ib : 32 * ib + 32, lanes].astype(F32)
                for t in range(9):
                    shift = level.stride * (t // 3 - 1) + t % 3 - 1
                    top = 288 * ib + 32 * t
                    cols[top : top + 32, :] = ahead(rows, shift).astype(BF)
            sums[:, lanes] = dot(weight[...], cols[...])
            return carry

        lax.fori_loop(0, level.planes // level.group, one, 0)

        def two(x, carry):
            def lanes(d):
                return pl.ds(pl.multiple_of((x + d) * n, n), n)

            total = sums[0:c, lanes(-1)] + sums[c : 2 * c, lanes(0)] + sums[2 * c : 3 * c, lanes(1)]
            dst[:, lanes(0)] = jnp.maximum(total, 0.0).astype(BF)
            return carry

        lax.fori_loop(1, level.planes - 1, two, 0)

    taps = k["taps"]
    g_ref = s["gathered"]
    own_rows = pl.ds(pl.multiple_of(yz * rs, rs), rs)
    for m, name in enumerate(("ba", "bb")):
        for ib in range(2):
            part = w[name][:, 864 * ib : 864 * ib + 864]
            g_ref[m, ib, own_rows, :] = dot(part, taps[...]).astype(BF)

    pack(FINE, raw_x, s["msg_x"])
    pl.semaphore_wait(barrier, len(greet))
    sent_x = exchange(FINE, raw_x, s["msg_x"], s["got_x"], s["ss"].at[0], s["rs"].at[0])

    def piece(ref, j):
        return ref.at[core, :, pl.ds(pl.multiple_of(j * rs, rs), rs), :]

    nsend = [0]
    waiting = {}

    def pass_on(j, key, peer):
        n = nsend[0]
        nsend[0] += 1
        waiting[key] = send(piece(g_ref, j), piece(g_ref, j), s["gs"].at[n], s["gr"].at[n], peer)

    me = yz
    if nzh == 2:
        pass_on(me, "z", z_peer)
    for d, peer in enumerate(y_peers):
        pass_on(me, ("y", 0, d), peer)

    for n, name in enumerate(("efa", "efb", "dfa", "dfb")):
        flat = dot(w[name][...], taps[...])
        for a in range(3):
            s["wf"][n, 32 * a : 32 * a + 32, :] = ahead(flat, 288 * a)[:, :288].astype(BF)
    lane = lax.broadcasted_iota(jnp.int32, (64, 896), 1)
    for n, name in enumerate(("ema", "emb", "dma", "dmb")):
        low = dot(w[name][:, 0:864], taps[...])
        high = dot(w[name][:, 864:1728], taps[...])
        for a in range(3):
            both = jnp.where(lane < 288, ahead(low, 288 * a), ahead(high, 288 * a - 288))
            s["wm"][n, 64 * a : 64 * a + 64, :] = both[:, :576].astype(BF)
    s["wr"][...] = dot(w["rf"][...], k["eight"][...]).astype(BF)
    for ib in range(2):
        s["wrm"][:, 256 * ib : 256 * ib + 256] = dot(
            w["rm"][:, 256 * ib : 256 * ib + 256], k["eight"][...]
        ).astype(BF)
    for name, table, into, wide in (("xf", "pick_fine", "wx", 256), ("xm", "pick_mid", "wxm", 512)):
        value = w[name][...].astype(F32)
        part = lax.broadcasted_iota(jnp.int32, value.shape, 1) % 4
        rows = jnp.concatenate([jnp.where(part == q, value, 0.0) for q in range(4)], axis=0)
        s[into][...] = dot_nt(k[table][...], rows.astype(BF)).astype(BF)

    if nzh == 2:
        waiting["z"].wait_recv()
        for d, peer in enumerate(y_peers):
            pass_on(at(1 - zh, gy, gxx), ("y", 1, d), peer)

    full_x, mid_f = s["full_x"], s["mid_f"]
    unpack(FINE, raw_x, s["got_x"], full_x, sent_x)
    conv(FINE, full_x, s["wf"].at[0], mid_f)
    raw_e0 = s["raw_e0"]
    conv(FINE, mid_f, s["wf"].at[1], s["e0"])

    def keep_inside(level, src, raw):
        n = level.lanes
        cells = lax.broadcasted_iota(jnp.int32, (1, n), 1)
        y, z = cells // level.stride - 2, cells % level.stride - 2
        inside = (y >= 0) & (y < level.extent) & (z >= 0) & (z < level.extent)
        for p in range(2, level.extent + 2):
            value = src[:, p * n : (p + 1) * n].astype(F32)
            raw[:, p * n : (p + 1) * n] = jnp.where(inside, value, 0.0).astype(BF)

    keep_inside(FINE, s["e0"], raw_e0)

    own = raw_e0[:, 512 : 14 * 256].astype(F32)
    for t in range(4):
        moved = ahead(own, 16 * (t // 2) + t % 2).astype(BF)
        for j in range(6):
            for a in range(2):
                top = 128 * a + 32 * t
                s["cols_r"][top : top + 32, 256 * j : 256 * j + 256] = moved[
                    :, 256 * (2 * j + a) : 256 * (2 * j + a) + 256
                ]
    wide = dot(s["wr"][...], s["cols_r"][...]).astype(BF)
    rows = jnp.concatenate([wide[:, 256 * j : 256 * j + 256] for j in range(6)], axis=0)
    small = dot(rows, k["down"][...]).astype(BF)
    raw_h1 = s["raw_h1"]
    for j in range(6):
        raw_h1[:, (j + 2) * 128 : (j + 3) * 128] = small[64 * j : 64 * j + 64]
    pack(MID, raw_h1, s["msg_h1"])
    sent_h1 = exchange(MID, raw_h1, s["msg_h1"], s["got_m"].at[0], s["ss"].at[1], s["rs"].at[1])
    pack(FINE, raw_e0, s["msg_e0"])
    sent_e0 = exchange(FINE, raw_e0, s["msg_e0"], s["got_e0"], s["ss"].at[2], s["rs"].at[2])

    for z in range(nzh):
        for d in range(ny - 1):
            waiting[("y", z, d)].wait_recv()
    zs = [zh, 1 - zh] if nzh == 2 else [zh]
    for n, z in enumerate(zs):
        for d in range(ny):
            j = at(z, (gy + d) % ny, gxx)
            pass_on(j, ("x+", n, d), x_next)
            if nx > 2:
                pass_on(j, ("x-", n, d), x_last)

    full_m, mid_m = s["full_m"], s["mid_m"]
    unpack(MID, raw_h1, s["got_m"].at[0], full_m, sent_h1)
    conv(MID, full_m, s["wm"].at[0], mid_m)
    conv(MID, mid_m, s["wm"].at[1], s["e1"])
    raw_e1 = s["raw_e1"]
    keep_inside(MID, s["e1"], raw_e1)

    own = raw_e1[:, 256 : 8 * 128].astype(F32)
    for t in range(4):
        moved = ahead(own, 10 * (t // 2) + t % 2).astype(BF)
        for j in range(3):
            for a in range(2):
                for ib in range(2):
                    top = 256 * ib + 128 * a + 32 * t
                    s["cols_rm"][top : top + 32, 128 * j : 128 * j + 128] = moved[
                        32 * ib : 32 * ib + 32, 128 * (2 * j + a) : 128 * (2 * j + a) + 128
                    ]
    wide = dot(s["wrm"][...], s["cols_rm"][...]).astype(BF)
    cells = dot(wide, k["down_bottom"][...])
    which = group_of(64, 32)
    tile = jnp.zeros((64, 128), F32)
    for q in range(4):
        tile = jnp.where(which == q, ahead(cells[64 * q : 64 * q + 64], -32 * q), tile)
    s["msg_b"][...] = tile.astype(BF)
    got_b = s["got_b"]
    got_b[13] = tile.astype(BF)
    sent_b = []
    for m, (a, b, c) in enumerate(ALL26):
        slot = 9 * (a + 1) + 3 * (b + 1) + c + 1
        sent_b.append(
            send(s["msg_b"], got_b.at[slot], s["ss"].at[3, m], s["rs"].at[3, m], device(a, b, c))
        )
    pack(MID, raw_e1, s["msg_e1"])
    sent_e1 = exchange(MID, raw_e1, s["msg_e1"], s["got_m"].at[1], s["ss"].at[4], s["rs"].at[4])

    for n in range(len(zs)):
        for d in range(ny):
            waiting[("x+", n, d)].wait_recv()
            if nx > 2:
                waiting[("x-", n, d)].wait_recv()
    far = []
    if nx > 2:
        for n, z in enumerate(zs):
            for d in range(ny):
                y = (gy + d) % ny
                if n == 0:
                    pass_on(at(z, y, (gxx + nx - 1) % nx), ("f", n, d), x_next)
                else:
                    pass_on(at(z, y, (gxx + 1) % nx), ("f", n, d), x_last)
                far.append(("f", n, d))
    for key in far:
        waiting[key].wait_recv()
    half = pltpu.make_async_remote_copy(
        src_ref=g_ref.at[core],
        dst_ref=g_ref.at[core],
        send_sem=s["ps"].at[0],
        recv_sem=s["ps"].at[1],
        device_id=partner,
        device_id_type=MESH,
    )
    half.start()

    for copy in sent_b:
        copy.wait_recv()
    for q in range(4):
        tiles = []
        for t in range(7):
            tile = jnp.zeros((64, 128), F32)
            for b in range(4):
                if 4 * t + b < 27:
                    tile = jnp.where(
                        which == b, ahead(got_b[4 * t + b].astype(F32), 32 * (q - b)), tile
                    )
            tiles.append(tile.astype(BF))
        s["b0"][64 * q : 64 * q + 64, :] = dot(jnp.concatenate(tiles, axis=1), k["blocks"][...]).astype(BF)
    half.wait()
    cols_b, acc = s["cols_b"], s["acc"]
    cols_b[864:896, :] = jnp.zeros((32, OUT1), BF)

    def bottom(src, m, dst, width):
        acc[:, :width] = jnp.zeros((256, width), F32)

        def one(kk, carry):
            rows = src[pl.ds(pl.multiple_of(kk * 32, 32), 32), :].astype(F32)
            for t in range(27):
                shift = 81 * (t // 9) + 9 * (t // 3 % 3) + t % 3
                cols_b[32 * t : 32 * t + 32, :width] = ahead(rows, shift)[:, :width].astype(BF)
            lhs = g_ref[m, kk % 2, pl.ds(pl.multiple_of(kk // 2 * 256, 256), 256), :]
            acc[:, :width] += dot(lhs, cols_b[:, :width])
            return carry

        lax.fori_loop(0, 8, one, 0)
        dst[...] = jnp.maximum(acc[:, :width], 0.0).astype(BF)

    bottom(s["b0"], 0, s["b1"], OUT1)
    bottom(s["b1"], 1, s["b2"], OUT2)

    full_e1 = s["full_e1"]
    unpack(MID, raw_e1, s["got_m"].at[1], full_e1, sent_e1)
    base = s["b2"][...].astype(F32)
    for j in range(5):
        spread = dot(ahead(base, 81 * j)[:, :128].astype(BF), k["up_mid"][...]).astype(BF)
        rows = jnp.concatenate([spread[:, 128 * q : 128 * q + 128] for q in range(4)], axis=0)
        risen = dot(s["wxm"][...], rows)
        for a in range(2):
            lanes = slice((2 * j + a) * 128, (2 * j + a + 1) * 128)
            total = risen[64 * a : 64 * a + 64] + full_e1[:, lanes].astype(F32)
            full_m[:, lanes] = total.astype(BF)
    conv(MID, full_m, s["wm"].at[2], mid_m)
    conv(MID, mid_m, s["wm"].at[3], s["f1"])
    raw_f1 = s["raw_f1"]
    keep_inside(MID, s["f1"], raw_f1)
    pack(MID, raw_f1, s["msg_f1"])
    sent_f1 = exchange(MID, raw_f1, s["msg_f1"], s["got_m"].at[2], s["ss"].at[5], s["rs"].at[5])

    full_e0 = s["full_e0"]
    unpack(FINE, raw_e0, s["got_e0"], full_e0, sent_e0)
    unpack(MID, raw_f1, s["got_m"].at[2], s["full_f1"], sent_f1)
    for j in range(8):
        spread = dot(s["full_f1"][:, (j + 1) * 128 : (j + 2) * 128], k["up_fine"][...]).astype(BF)
        rows = jnp.concatenate([spread[:, 256 * q : 256 * q + 256] for q in range(4)], axis=0)
        risen = dot(s["wx"][...], rows)
        for a in range(2):
            lanes = slice((2 * j + a) * 256, (2 * j + a + 1) * 256)
            total = risen[32 * a : 32 * a + 32] + full_e0[:, lanes].astype(F32)
            full_x[:, lanes] = total.astype(BF)
    conv(FINE, full_x, s["wf"].at[2], mid_f)
    conv(FINE, mid_f, s["wf"].at[3], s["e0"])
    rows = jnp.concatenate([s["e0"][:, (p + 2) * 256 : (p + 3) * 256] for p in range(12)], axis=0)
    out_ref[...] = dot(rows, k["leave"][...])[:, :144].astype(BF)
    for copy in started:
        copy.wait_send()


def scratch(nyz, place_of):
    nzh, ny, nx = place_of
    fine, mid = (32, 16 * 256), (64, 10 * 128)
    count = 1 + nzh * (ny - 1) + 3 * nzh * ny
    vm = lambda *shape: pltpu.VMEM(shape, BF)
    return dict(
        raw_x=vm(*fine), full_x=vm(*fine), mid_f=vm(*fine), e0=vm(*fine), raw_e0=vm(*fine), full_e0=vm(*fine),
        raw_h1=vm(*mid), full_m=vm(*mid), mid_m=vm(*mid), e1=vm(*mid), raw_e1=vm(*mid), full_e1=vm(*mid),
        f1=vm(*mid), raw_f1=vm(*mid), full_f1=vm(*mid),
        msg_x=vm(8, 3, 32, 128), msg_e0=vm(8, 3, 32, 128), got_x=vm(3, 8, 3, 32, 128), got_e0=vm(3, 8, 3, 32, 128),
        msg_h1=vm(8, 1, 64, 128), msg_e1=vm(8, 1, 64, 128), msg_f1=vm(8, 1, 64, 128), got_m=vm(3, 3, 8, 1, 64, 128),
        msg_b=vm(64, 128), got_b=vm(27, 64, 128),
        b0=vm(256, FLAT), b1=vm(256, OUT1), b2=vm(256, OUT2),
        wf=vm(4, 96, 288), wm=vm(4, 192, 576), wr=vm(64, 256), wrm=vm(256, 512), wx=vm(64, 256), wxm=vm(128, 1024),
        gathered=vm(2, 2, 1024, 896),
        cols_f=vm(288, 1024), cols_m=vm(576, 640), cols_r=vm(256, 1536), cols_rm=vm(512, 384), cols_b=vm(896, OUT1),
        sums_f=pltpu.VMEM((96, 16 * 256), F32), sums_m=pltpu.VMEM((192, 1280), F32), acc=pltpu.VMEM((256, OUT1), F32),
        ss=pltpu.SemaphoreType.DMA((6, 26)), rs=pltpu.SemaphoreType.DMA((6, 26)),
        gs=pltpu.SemaphoreType.DMA((count,)), gr=pltpu.SemaphoreType.DMA((count,)), ps=pltpu.SemaphoreType.DMA((2,)),
    )


SCRATCH = tuple(scratch(64, (2, 8, 4)))


def solution(mesh):
    ngx, nyz = mesh.shape["gx"], mesh.shape["yz"]
    place_of = (2, 8, 4) if nyz == 64 else (1, math.isqrt(nyz), math.isqrt(nyz))
    tables = {name: np.asarray(value, BF) for name, value in constants().items()}

    def body(features_in, *weights):
        planes = features_in[0].transpose(1, 0, 2).reshape(384, 144)
        result = pl.pallas_call(
            lambda *refs: kernel(ngx, nyz, place_of, *refs),
            name="unet",
            out_shape=jax.ShapeDtypeStruct((384, 144), BF),
            in_specs=[pl.BlockSpec(memory_space=pltpu.VMEM)] * (1 + len(NAMES) + len(CONST)),
            out_specs=pl.BlockSpec(memory_space=pltpu.VMEM),
            scratch_shapes=list(scratch(nyz, place_of).values()),
            compiler_params=pltpu.CompilerParams(
                collective_id=0, has_side_effects=True, vmem_limit_bytes=60 * 2**20
            ),
        )(planes, *weights, *(jnp.asarray(tables[name]) for name in CONST))
        return result.reshape(12, 32, 144).transpose(1, 0, 2)[None]

    placed = tuple(
        P("yz", None, "gx", None) if i == 0 else P("yz", None) if i in (7, 8) else P() for i in range(15)
    )
    return jax.shard_map(
        body, mesh=mesh, in_specs=placed, out_specs=P("yz", None, "gx", None), check_vma=False
    )
```

time: 674 us -> 138 us (0.20)
  the two profiles are of different devices: /device:TPU:62 before, /device:TPU:1 now
where the time goes in v1:
time: 138 us; the launch traced here: 136 us
  Pallas kernels  134 us (97%)
  local copies, waits for them, and re-layouts  1.62 us (1%)
    pallas_call x1, Pallas kernels, body(): pl.pallas_call(lambda *refs: kernel(ngx, nyz, place_of, *refs), name='une...  134 us

profile of v1, /device:TPU:1, one launch (start us, length us, event | category | flops | bytes accessed | tf_op | source)
XLA Modules:
  0.0 135.5 jit_solution(17650457978727095752)
XLA Ops:
  0.0 133.9 %unet.1 = bf16[384,144]{1,0:T(8,128)(2,1)} custom-call(bf16[384,144]{1,0:T(8,128)(2,1)} %bitcast.11, bf16[32,864]{1,0:T(8,128)(2,1)} %refs_1_.1, bf16[32,864]{1,0:T(8,128)(2,1)} %refs_2_.1, bf16[64,256]{1,0:T(8,128)(2,1)} %refs_3_.1, bf16[64,1728]{1,0:T(8,128)(2,1)} %refs_4_.1, bf16[64,1728]{1,0:T(8,128)(2,1)} %refs_5_.1, bf16[256,512]{1,0:T(8,128)(2,1)} %refs_6_.1, ...), custom_call_target="tpu_custom_call" | custom-call | tf_op jit(solution)/shard_map/unet/pallas_call | solution.py:579
  133.9 1.6 %copy.32 = bf16[1,32,12,144]{3,1,2,0:T(8,128)(2,1)} copy(bf16[1,32,12,144]{3,1,2,0:T(8,128)(2,1)} %bitcast.10) | data formatting | bytes 221184

commit v2 on v1

--- a/solution.py
+++ b/solution.py
@@ -21,6 +21,9 @@
 ]
 
 
+CORNERS = [d for d, (b, c) in enumerate(YZ8) if b and c]
+
+
 class Level:
     def __init__(self, width, extent, stride, lanes, group):
         self.width, self.extent, self.stride, self.lanes = width, extent, stride, lanes
@@ -29,6 +32,8 @@
         self.per_tile = 128 // self.share
         self.tiles = -(-extent // self.per_tile)
         self.group = group
+        self.fold = width // 16
+        self.span = 128 // self.fold
 
     def lane(self, y, z):
         return (y + 2) * self.stride + z + 2
@@ -62,10 +67,6 @@
     for y in range(12):
         for z in range(12):
             place[y * 12 + z, FINE.lane(y, z)] = 1
-    taps = np.zeros((864, 896), np.float32)
-    for i in range(32):
-        for t in range(27):
-            taps[27 * i + t, 32 * t + i] = 1
     eight = np.zeros((256, 256), np.float32)
     for i in range(32):
         for t in range(8):
@@ -89,14 +90,6 @@
         for z in range(10):
             part = 2 * (y % 2) + z % 2
             up_mid[9 * (y // 2) + z // 2, 128 * part + 10 * y + z] = 1
-    blocks = np.zeros((FLAT, FLAT), np.float32)
-    for a in (-1, 0, 1):
-        for b in (-1, 0, 1):
-            for c in (-1, 0, 1):
-                row = 32 * (9 * (a + 1) + 3 * (b + 1) + c + 1)
-                for i in range(27):
-                    x, y, z = i // 9 - 3 * a + 3, i // 3 % 3 - 3 * b + 3, i % 3 - 3 * c + 3
-                    blocks[row + i, 81 * x + 9 * y + z] = 1
     pick = []
     for width in (32, 64):
         table = np.zeros((2 * width, 8 * width), np.float32)
@@ -110,13 +103,11 @@
     return dict(
         place=place,
         leave=np.pad(place.T, ((0, 0), (0, 112))),
-        taps=taps,
         eight=eight,
         down=down,
         down_bottom=down_bottom,
         up_fine=up_fine,
         up_mid=up_mid,
-        blocks=blocks,
         pick_fine=pick[0],
         pick_mid=pick[1],
         fine_pack=fine_pack,
@@ -188,6 +179,9 @@
     for peer in greet:
         pl.semaphore_signal(barrier, inc=1, device_id=peer, device_id_type=MESH)
 
+    def box_of(name):
+        return {part: s[name + "_" + part] for part in ("face", "wing", "corner", "end") if name + "_" + part in s}
+
     started = []
 
     def send(src, dst, ssem, rsem, peer):
@@ -208,10 +202,23 @@
     for p in range(12):
         raw_x[:, (p + 2) * 256 : (p + 3) * 256] = planes[32 * p : 32 * p + 32]
 
-    def pack(level, raw, message):
+    def folded(level, value, start):
+        which = group_of(16, level.span)
+        tile = jnp.zeros((16, 128), F32)
+        for h in range(level.fold):
+            tile = jnp.where(which == h, ahead(value[16 * h : 16 * h + 16], start - level.span * h), tile)
+        return tile.astype(BF)
+
+    def unfolded(level, value, start):
+        value = value.astype(F32)
+        return jnp.concatenate([ahead(value, level.span * h - start) for h in range(level.fold)], axis=0)
+
+    def pack(level, raw, box):
         c, e, n = level.width, level.extent, level.lanes
         table = k["fine_pack" if level is FINE else "mid_pack"]
         which = group_of(c, level.share)
+        which4 = group_of(c, 4)
+        corners = [jnp.zeros((c, 128), F32)] * 8
         for t in range(level.tiles):
             members = range(t * level.per_tile, min(e, (t + 1) * level.per_tile))
             rows = jnp.concatenate([raw[:, (p + 2) * n : (p + 3) * n] for p in members], axis=0)
@@ -219,53 +226,87 @@
             for d in range(8):
                 half, base = divmod(d * level.share, 128)
                 tile = jnp.zeros((c, 128), F32)
-                for q in range(len(members)):
+                for q, p in enumerate(members):
                     part = faces[q * c : (q + 1) * c, 128 * half : 128 * half + 128]
                     tile = jnp.where(which == q, ahead(part, base - q * level.share), tile)
-                message[d, t] = tile.astype(BF)
-
-    def exchange(level, raw, message, arrived, ssem, rsem):
+                    if d in CORNERS:
+                        corners[d] = jnp.where(which4 == p, ahead(part, base - 4 * p), corners[d])
+                if d not in CORNERS:
+                    box["face"][d, t] = tile.astype(BF)
+                if t == level.tiles - 1:
+                    box["wing"][1, d] = folded(level, tile, 64)
+                if t == 0:
+                    box["wing"][0, d] = folded(level, tile, 0)
+        for d in CORNERS:
+            box["corner"][d] = folded(level, corners[d], 0)
+        if level is MID:
+            low = lax.broadcasted_iota(jnp.int32, (c, 128), 1) < 64
+            for side, first in ((1, e), (0, 2)):
+                a = raw[:, first * n : (first + 1) * n].astype(F32)
+                b = raw[:, (first + 1) * n : (first + 2) * n].astype(F32)
+                box["end"][side] = jnp.where(low, ahead(a, 22), ahead(b, 22 - 64)).astype(BF)
+
+    def exchange(level, raw, box, got, ssem, rsem):
         n, e = level.lanes, level.extent
         copies = []
         for m, (a, b, c) in enumerate(ALL26):
+            side = 1 if a == 1 else 0
             if (b, c) == (0, 0):
-                src = raw.at[:, (e * n if a == 1 else 2 * n) : (e * n if a == 1 else 2 * n) + 2 * n]
-                dst = raw.at[:, 0 : 2 * n] if a == 1 else raw.at[:, (e + 2) * n : (e + 4) * n]
+                if level is MID:
+                    src, dst = box["end"].at[side], got["end"].at[side]
+                elif a == 1:
+                    src, dst = raw.at[:, e * n : (e + 2) * n], raw.at[:, 0 : 2 * n]
+                else:
+                    src, dst = raw.at[:, 2 * n : 4 * n], raw.at[:, (e + 2) * n : (e + 4) * n]
             else:
                 d = YZ8.index((b, c))
-                if a == 0:
-                    src, dst = message.at[d], arrived.at[1, d]
+                if a != 0:
+                    src, dst = box["wing"].at[side, d], got["wing"].at[side, d]
+                elif d in CORNERS:
+                    src, dst = box["corner"].at[d], got["corner"].at[d]
                 else:
-                    src = message.at[d, level.tiles - 1 if a == 1 else 0]
-                    dst = arrived.at[2 if a == 1 else 0, d, 0]
+                    src, dst = box["face"].at[d], got["face"].at[d]
             copies.append(send(src, dst, ssem.at[m], rsem.at[m], device(a, b, c)))
         return copies
 
-    def unpack(level, raw, arrived, full, copies):
+    def unpack(level, raw, got, full, copies):
         c, e, n = level.width, level.extent, level.lanes
         table = k["fine_unpack" if level is FINE else "mid_unpack"]
         which = group_of(c, level.share)
         for copy in copies:
             copy.wait_recv()
+        if level is MID:
+            lane = lax.broadcasted_iota(jnp.int32, (c, 128), 1)
+            mine = (lane >= 22) & (lane < 86)
+            for side, first in ((1, 0), (0, e + 2)):
+                value = got["end"][side].astype(F32)
+                for q in range(2):
+                    lanes = slice((first + q) * n, (first + q + 1) * n)
+                    raw[:, lanes] = jnp.where(mine, ahead(value, 64 * q - 22), 0.0).astype(BF)
+        corner = {d: unfolded(level, got["corner"][d], 0) for d in CORNERS}
+        wing = {
+            (side, d): unfolded(level, got["wing"][side, d], 64 * side) for side in range(2) for d in range(8)
+        }
 
         def halo(plane):
             p = plane - 2
-            slot, tile = 1, p // level.per_tile
-            if p < 0:
-                slot, tile, p = 2, 0, p + e
-            elif p >= e:
-                slot, tile, p = 0, 0, p - e
-            q = p % level.per_tile
             halves = []
             for half in range(n // 128):
                 value = jnp.zeros((c, 128), F32)
                 for d in range(8):
-                    if d * level.share // 128 == half:
-                        base = d * level.share % 128
-                        piece = arrived[slot, d, tile].astype(F32)
-                        value = jnp.where(
-                            which == base // level.share, ahead(piece, q * level.share - base), value
-                        )
+                    if d * level.share // 128 != half:
+                        continue
+                    base = d * level.share % 128
+                    if p < 0:
+                        piece, start = wing[1, d], (p + e) % level.per_tile * level.share
+                    elif p >= e:
+                        piece, start = wing[0, d], (p - e) * level.share
+                    elif d in CORNERS:
+                        piece, start = corner[d], 4 * p
+                    else:
+                        piece = got["face"][d, p // level.per_tile].astype(F32)
+                        start = p % level.per_tile * level.share
+                    value = jnp.where(which == base // level.share, ahead(piece, start - base), value)
                 halves.append(value)
             return jnp.concatenate(halves, axis=1) if len(halves) > 1 else halves[0]
 
@@ -306,7 +347,16 @@
 
         lax.fori_loop(1, level.planes - 1, two, 0)
 
-    taps = k["taps"]
+    taps = s["taps"]
+    column = lax.broadcasted_iota(jnp.int32, (1, 896), 1)
+    wanted = jnp.where(column < 864, 27 * (column & 31) + (column >> 5), -1)
+    row = lax.broadcasted_iota(jnp.int32, (32, 896), 0)
+
+    def tap_rows(n, carry):
+        taps[pl.ds(pl.multiple_of(n * 32, 32), 32), :] = jnp.where(row + 32 * n == wanted, 1.0, 0.0).astype(BF)
+        return carry
+
+    lax.fori_loop(0, 27, tap_rows, 0)
     g_ref = s["gathered"]
     own_rows = pl.ds(pl.multiple_of(yz * rs, rs), rs)
     for m, name in enumerate(("ba", "bb")):
@@ -314,9 +364,9 @@
             part = w[name][:, 864 * ib : 864 * ib + 864]
             g_ref[m, ib, own_rows, :] = dot(part, taps[...]).astype(BF)
 
-    pack(FINE, raw_x, s["msg_x"])
+    pack(FINE, raw_x, box_of("msg_x"))
     pl.semaphore_wait(barrier, len(greet))
-    sent_x = exchange(FINE, raw_x, s["msg_x"], s["got_x"], s["ss"].at[0], s["rs"].at[0])
+    sent_x = exchange(FINE, raw_x, box_of("msg_x"), box_of("got_x"), s["ss"].at[0], s["rs"].at[0])
 
     def piece(ref, j):
         return ref.at[core, :, pl.ds(pl.multiple_of(j * rs, rs), rs), :]
@@ -329,11 +379,24 @@
         nsend[0] += 1
         waiting[key] = send(piece(g_ref, j), piece(g_ref, j), s["gs"].at[n], s["gr"].at[n], peer)
 
-    me = yz
+    zs = [zh, 1 - zh] if nzh == 2 else [zh]
+
+    def along_y(i):
+        for d, peer in enumerate(y_peers):
+            pass_on(at(zs[i], gy, gxx), ("y", i, d + 1), peer)
+
+    def along_x(i, d, local):
+        j = at(zs[i], (gy - d + ny) % ny, gxx)
+        pass_on(j, ("x+", i, d), x_next)
+        if nx > 2:
+            pass_on(j, ("x-", i, d), x_last)
+        if not local:
+            pass_on(j, ("p", i, d, 0), partner)
+
     if nzh == 2:
-        pass_on(me, "z", z_peer)
-    for d, peer in enumerate(y_peers):
-        pass_on(me, ("y", 0, d), peer)
+        pass_on(yz, "z", z_peer)
+    along_y(0)
+    along_x(0, 0, True)
 
     for n, name in enumerate(("efa", "efb", "dfa", "dfb")):
         flat = dot(w[name][...], taps[...])
@@ -357,13 +420,34 @@
         rows = jnp.concatenate([jnp.where(part == q, value, 0.0) for q in range(4)], axis=0)
         s[into][...] = dot_nt(k[table][...], rows.astype(BF)).astype(BF)
 
+    column = lax.broadcasted_iota(jnp.int32, (32, FLAT), 1)
+    cell = lax.broadcasted_iota(jnp.int32, (32, 1), 0)
+    cx = (cell * 57) >> 9
+    cy = ((cell - 9 * cx) * 11) >> 5
+    offset = jnp.where(cell < 27, 72 * cx + 6 * cy + cell, -4096)
+    blocks = s["blocks"]
+    blocks[864:896, :] = jnp.zeros((32, FLAT), BF)
+
+    def block_rows(b, carry):
+        first = 81 * 3 * (2 - b // 9) + 9 * 3 * (2 - b // 3 % 3) + 3 * (2 - b % 3)
+        blocks[pl.ds(pl.multiple_of(b * 32, 32), 32), :] = jnp.where(column == offset + first, 1.0, 0.0).astype(BF)
+        return carry
+
+    lax.fori_loop(0, 27, block_rows, 0)
+
+    def step_y(i):
+        for d in sorted(range(1, ny), key=lambda d: min(d, ny - d)):
+            waiting["y", i, d].wait_recv()
+            along_x(i, d, False)
+
     if nzh == 2:
         waiting["z"].wait_recv()
-        for d, peer in enumerate(y_peers):
-            pass_on(at(1 - zh, gy, gxx), ("y", 1, d), peer)
+        along_y(1)
+        along_x(1, 0, False)
 
     full_x, mid_f = s["full_x"], s["mid_f"]
-    unpack(FINE, raw_x, s["got_x"], full_x, sent_x)
+    step_y(0)
+    unpack(FINE, raw_x, box_of("got_x"), full_x, sent_x)
     conv(FINE, full_x, s["wf"].at[0], mid_f)
     raw_e0 = s["raw_e0"]
     conv(FINE, mid_f, s["wf"].at[1], s["e0"])
@@ -394,24 +478,13 @@
     raw_h1 = s["raw_h1"]
     for j in range(6):
         raw_h1[:, (j + 2) * 128 : (j + 3) * 128] = small[64 * j : 64 * j + 64]
-    pack(MID, raw_h1, s["msg_h1"])
-    sent_h1 = exchange(MID, raw_h1, s["msg_h1"], s["got_m"].at[0], s["ss"].at[1], s["rs"].at[1])
-    pack(FINE, raw_e0, s["msg_e0"])
-    sent_e0 = exchange(FINE, raw_e0, s["msg_e0"], s["got_e0"], s["ss"].at[2], s["rs"].at[2])
-
-    for z in range(nzh):
-        for d in range(ny - 1):
-            waiting[("y", z, d)].wait_recv()
-    zs = [zh, 1 - zh] if nzh == 2 else [zh]
-    for n, z in enumerate(zs):
-        for d in range(ny):
-            j = at(z, (gy + d) % ny, gxx)
-            pass_on(j, ("x+", n, d), x_next)
-            if nx > 2:
-                pass_on(j, ("x-", n, d), x_last)
+    pack(MID, raw_h1, box_of("msg_h1"))
+    sent_h1 = exchange(MID, raw_h1, box_of("msg_h1"), box_of("got_h1"), s["ss"].at[1], s["rs"].at[1])
+    if nzh == 2:
+        step_y(1)
 
     full_m, mid_m = s["full_m"], s["mid_m"]
-    unpack(MID, raw_h1, s["got_m"].at[0], full_m, sent_h1)
+    unpack(MID, raw_h1, box_of("got_h1"), full_m, sent_h1)
     conv(MID, full_m, s["wm"].at[0], mid_m)
     conv(MID, mid_m, s["wm"].at[1], s["e1"])
     raw_e1 = s["raw_e1"]
@@ -442,35 +515,29 @@
         sent_b.append(
             send(s["msg_b"], got_b.at[slot], s["ss"].at[3, m], s["rs"].at[3, m], device(a, b, c))
         )
-    pack(MID, raw_e1, s["msg_e1"])
-    sent_e1 = exchange(MID, raw_e1, s["msg_e1"], s["got_m"].at[1], s["ss"].at[4], s["rs"].at[4])
-
-    for n in range(len(zs)):
-        for d in range(ny):
-            waiting[("x+", n, d)].wait_recv()
-            if nx > 2:
-                waiting[("x-", n, d)].wait_recv()
-    far = []
+    pack(MID, raw_e1, box_of("msg_e1"))
+    sent_e1 = exchange(MID, raw_e1, box_of("msg_e1"), box_of("got_e1"), s["ss"].at[4], s["rs"].at[4])
+
+    order = [(i, d) for i in range(nzh) for d in sorted(range(ny), key=lambda d: min(d, ny - d))]
+    for i, d in order:
+        y = (gy - d + ny) % ny
+        waiting["x+", i, d].wait_recv()
+        j = at(zs[i], y, (gxx + nx - 1) % nx)
+        if nx > 2 and i == 0:
+            pass_on(j, ("f", i, d), x_next)
+        pass_on(j, ("p", i, d, 1), partner)
+        if nx > 2:
+            waiting["x-", i, d].wait_recv()
+            j = at(zs[i], y, (gxx + 1) % nx)
+            if i == 1:
+                pass_on(j, ("f", i, d), x_last)
+            pass_on(j, ("p", i, d, 2), partner)
+    pack(FINE, raw_e0, box_of("msg_e0"))
+    sent_e0 = exchange(FINE, raw_e0, box_of("msg_e0"), box_of("got_e0"), s["ss"].at[2], s["rs"].at[2])
     if nx > 2:
-        for n, z in enumerate(zs):
-            for d in range(ny):
-                y = (gy + d) % ny
-                if n == 0:
-                    pass_on(at(z, y, (gxx + nx - 1) % nx), ("f", n, d), x_next)
-                else:
-                    pass_on(at(z, y, (gxx + 1) % nx), ("f", n, d), x_last)
-                far.append(("f", n, d))
-    for key in far:
-        waiting[key].wait_recv()
-    half = pltpu.make_async_remote_copy(
-        src_ref=g_ref.at[core],
-        dst_ref=g_ref.at[core],
-        send_sem=s["ps"].at[0],
-        recv_sem=s["ps"].at[1],
-        device_id=partner,
-        device_id_type=MESH,
-    )
-    half.start()
+        for i, d in order:
+            waiting["f", i, d].wait_recv()
+            pass_on(at(zs[i], (gy - d + ny) % ny, (gxx + 2) % nx), ("p", i, d, 3), partner)
 
     for copy in sent_b:
         copy.wait_recv()
@@ -484,8 +551,10 @@
                         which == b, ahead(got_b[4 * t + b].astype(F32), 32 * (q - b)), tile
                     )
             tiles.append(tile.astype(BF))
-        s["b0"][64 * q : 64 * q + 64, :] = dot(jnp.concatenate(tiles, axis=1), k["blocks"][...]).astype(BF)
-    half.wait()
+        s["b0"][64 * q : 64 * q + 64, :] = dot(jnp.concatenate(tiles, axis=1), blocks[...]).astype(BF)
+    for key, copy in waiting.items():
+        if key[0] == "p":
+            copy.wait_recv()
     cols_b, acc = s["cols_b"], s["acc"]
     cols_b[864:896, :] = jnp.zeros((32, OUT1), BF)
 
@@ -508,7 +577,7 @@
     bottom(s["b1"], 1, s["b2"], OUT2)
 
     full_e1 = s["full_e1"]
-    unpack(MID, raw_e1, s["got_m"].at[1], full_e1, sent_e1)
+    unpack(MID, raw_e1, box_of("got_e1"), full_e1, sent_e1)
     base = s["b2"][...].astype(F32)
     for j in range(5):
         spread = dot(ahead(base, 81 * j)[:, :128].astype(BF), k["up_mid"][...]).astype(BF)
@@ -522,12 +591,12 @@
     conv(MID, mid_m, s["wm"].at[3], s["f1"])
     raw_f1 = s["raw_f1"]
     keep_inside(MID, s["f1"], raw_f1)
-    pack(MID, raw_f1, s["msg_f1"])
-    sent_f1 = exchange(MID, raw_f1, s["msg_f1"], s["got_m"].at[2], s["ss"].at[5], s["rs"].at[5])
+    pack(MID, raw_f1, box_of("msg_f1"))
+    sent_f1 = exchange(MID, raw_f1, box_of("msg_f1"), box_of("got_f1"), s["ss"].at[5], s["rs"].at[5])
 
     full_e0 = s["full_e0"]
-    unpack(FINE, raw_e0, s["got_e0"], full_e0, sent_e0)
-    unpack(MID, raw_f1, s["got_m"].at[2], s["full_f1"], sent_f1)
+    unpack(FINE, raw_e0, box_of("got_e0"), full_e0, sent_e0)
+    unpack(MID, raw_f1, box_of("got_f1"), s["full_f1"], sent_f1)
     for j in range(8):
         spread = dot(s["full_f1"][:, (j + 1) * 128 : (j + 2) * 128], k["up_fine"][...]).astype(BF)
         rows = jnp.concatenate([spread[:, 256 * q : 256 * q + 256] for q in range(4)], axis=0)
@@ -547,18 +616,28 @@
 def scratch(nyz, place_of):
     nzh, ny, nx = place_of
     fine, mid = (32, 16 * 256), (64, 10 * 128)
-    count = 1 + nzh * (ny - 1) + 3 * nzh * ny
+    count = 1 + nzh * (ny - 1) + 3 * nzh * ny + nyz
     vm = lambda *shape: pltpu.VMEM(shape, BF)
     return dict(
         raw_x=vm(*fine), full_x=vm(*fine), mid_f=vm(*fine), e0=vm(*fine), raw_e0=vm(*fine), full_e0=vm(*fine),
         raw_h1=vm(*mid), full_m=vm(*mid), mid_m=vm(*mid), e1=vm(*mid), raw_e1=vm(*mid), full_e1=vm(*mid),
         f1=vm(*mid), raw_f1=vm(*mid), full_f1=vm(*mid),
-        msg_x=vm(8, 3, 32, 128), msg_e0=vm(8, 3, 32, 128), got_x=vm(3, 8, 3, 32, 128), got_e0=vm(3, 8, 3, 32, 128),
-        msg_h1=vm(8, 1, 64, 128), msg_e1=vm(8, 1, 64, 128), msg_f1=vm(8, 1, 64, 128), got_m=vm(3, 3, 8, 1, 64, 128),
+        **{
+            f"{way}_{name}_{part}": vm(*shape)
+            for way in ("msg", "got")
+            for name in ("x", "e0", "h1", "e1", "f1")
+            for part, shape in dict(
+                face=(8, 3, 32, 128) if name in ("x", "e0") else (8, 1, 64, 128),
+                wing=(2, 8, 16, 128),
+                corner=(8, 16, 128),
+                end=(2, 64, 128),
+            ).items()
+            if part != "end" or name not in ("x", "e0")
+        },
         msg_b=vm(64, 128), got_b=vm(27, 64, 128),
         b0=vm(256, FLAT), b1=vm(256, OUT1), b2=vm(256, OUT2),
         wf=vm(4, 96, 288), wm=vm(4, 192, 576), wr=vm(64, 256), wrm=vm(256, 512), wx=vm(64, 256), wxm=vm(128, 1024),
-        gathered=vm(2, 2, 1024, 896),
+        gathered=vm(2, 2, 1024, 896), taps=vm(864, 896), blocks=vm(FLAT, FLAT),
         cols_f=vm(288, 1024), cols_m=vm(576, 640), cols_r=vm(256, 1536), cols_rm=vm(512, 384), cols_b=vm(896, OUT1),
         sums_f=pltpu.VMEM((96, 16 * 256), F32), sums_m=pltpu.VMEM((192, 1280), F32), acc=pltpu.VMEM((256, OUT1), F32),
         ss=pltpu.SemaphoreType.DMA((6, 26)), rs=pltpu.SemaphoreType.DMA((6, 26)),

time: 138 us -> 109 us (0.79); the launches traced: 136 us -> 109 us
  Pallas kernels: 134 us -> 107 us
    pallas_call x1, Pallas kernels: 134 us -> 107 us  [body(): pl.pallas_call(lambda *refs: kernel(ngx, nyz, place_of, *refs), name='une...]
where the time goes in v2:
time: 109 us
  Pallas kernels  107 us (98%)
  local copies, waits for them, and re-layouts  1.62 us (1%)
    pallas_call x1, Pallas kernels, body(): pl.pallas_call(lambda *refs: kernel(ngx, nyz, place_of, *refs), name='une...  107 us

profile of v2, /device:TPU:1, one launch (start us, length us, event | category | flops | bytes accessed | tf_op | source)
XLA Modules:
  0.0 108.5 jit_solution(8745953996991699904)
XLA Ops:
  0.0 106.9 %unet.1 = bf16[384,144]{1,0:T(8,128)(2,1)} custom-call(bf16[384,144]{1,0:T(8,128)(2,1)} %bitcast.11, bf16[32,864]{1,0:T(8,128)(2,1)} %refs_1_.1, bf16[32,864]{1,0:T(8,128)(2,1)} %refs_2_.1, bf16[64,256]{1,0:T(8,128)(2,1)} %refs_3_.1, bf16[64,1728]{1,0:T(8,128)(2,1)} %refs_4_.1, bf16[64,1728]{1,0:T(8,128)(2,1)} %refs_5_.1, bf16[256,512]{1,0:T(8,128)(2,1)} %refs_6_.1, ...), custom_call_target="tpu_custom_call" | custom-call | tf_op jit(solution)/shard_map/unet/pallas_call | solution.py:658
  106.9 1.6 %copy.30 = bf16[1,32,12,144]{3,1,2,0:T(8,128)(2,1)} copy(bf16[1,32,12,144]{3,1,2,0:T(8,128)(2,1)} %bitcast.10) | data formatting | bytes 221184

commit v3 on v2

--- a/solution.py
+++ b/solution.py
@@ -168,12 +168,13 @@
         return z * ny * nx + y * nx + x
 
     z_peer = ((ngx // 2 - 1 - gx // 2) * 2 + core, at(1 - zh, gy, gxx))
-    y_peers = [(gx, at(zh, (gy + d) % ny, gxx)) for d in range(1, ny)]
+    y_next = (gx, at(zh, (gy + 1) % ny, gxx))
+    y_last = (gx, at(zh, (gy + ny - 1) % ny, gxx))
     x_next = (gx, at(zh, gy, (gxx + 1) % nx))
     x_last = (gx, at(zh, gy, (gxx + nx - 1) % nx))
 
     barrier = pltpu.get_barrier_semaphore()
-    greet = [device(*d) for d in ALL26] + y_peers + [x_next, x_last, partner]
+    greet = [device(*d) for d in ALL26] + [y_next, y_last, x_next, x_last, partner]
     if nzh == 2:
         greet.append(z_peer)
     for peer in greet:
@@ -204,13 +205,12 @@
 
     def folded(level, value, start):
         which = group_of(16, level.span)
-        tile = jnp.zeros((16, 128), F32)
+        tile = jnp.zeros((16, 128), BF)
         for h in range(level.fold):
             tile = jnp.where(which == h, ahead(value[16 * h : 16 * h + 16], start - level.span * h), tile)
-        return tile.astype(BF)
+        return tile
 
     def unfolded(level, value, start):
-        value = value.astype(F32)
         return jnp.concatenate([ahead(value, level.span * h - start) for h in range(level.fold)], axis=0)
 
     def pack(level, raw, box):
@@ -218,21 +218,21 @@
         table = k["fine_pack" if level is FINE else "mid_pack"]
         which = group_of(c, level.share)
         which4 = group_of(c, 4)
-        corners = [jnp.zeros((c, 128), F32)] * 8
+        corners = [jnp.zeros((c, 128), BF)] * 8
         for t in range(level.tiles):
             members = range(t * level.per_tile, min(e, (t + 1) * level.per_tile))
             rows = jnp.concatenate([raw[:, (p + 2) * n : (p + 3) * n] for p in members], axis=0)
-            faces = dot(rows, table[...])
+            faces = dot(rows, table[...]).astype(BF)
             for d in range(8):
                 half, base = divmod(d * level.share, 128)
-                tile = jnp.zeros((c, 128), F32)
+                tile = jnp.zeros((c, 128), BF)
                 for q, p in enumerate(members):
                     part = faces[q * c : (q + 1) * c, 128 * half : 128 * half + 128]
                     tile = jnp.where(which == q, ahead(part, base - q * level.share), tile)
                     if d in CORNERS:
                         corners[d] = jnp.where(which4 == p, ahead(part, base - 4 * p), corners[d])
                 if d not in CORNERS:
-                    box["face"][d, t] = tile.astype(BF)
+                    box["face"][d, t] = tile
                 if t == level.tiles - 1:
                     box["wing"][1, d] = folded(level, tile, 64)
                 if t == 0:
@@ -242,9 +242,9 @@
         if level is MID:
             low = lax.broadcasted_iota(jnp.int32, (c, 128), 1) < 64
             for side, first in ((1, e), (0, 2)):
-                a = raw[:, first * n : (first + 1) * n].astype(F32)
-                b = raw[:, (first + 1) * n : (first + 2) * n].astype(F32)
-                box["end"][side] = jnp.where(low, ahead(a, 22), ahead(b, 22 - 64)).astype(BF)
+                a = raw[:, first * n : (first + 1) * n]
+                b = raw[:, (first + 1) * n : (first + 2) * n]
+                box["end"][side] = jnp.where(low, ahead(a, 22), ahead(b, 22 - 64))
 
     def exchange(level, raw, box, got, ssem, rsem):
         n, e = level.lanes, level.extent
@@ -278,11 +278,12 @@
         if level is MID:
             lane = lax.broadcasted_iota(jnp.int32, (c, 128), 1)
             mine = (lane >= 22) & (lane < 86)
+            zero = jnp.zeros((c, 128), BF)
             for side, first in ((1, 0), (0, e + 2)):
-                value = got["end"][side].astype(F32)
+                value = got["end"][side]
                 for q in range(2):
                     lanes = slice((first + q) * n, (first + q + 1) * n)
-                    raw[:, lanes] = jnp.where(mine, ahead(value, 64 * q - 22), 0.0).astype(BF)
+                    raw[:, lanes] = jnp.where(mine, ahead(value, 64 * q - 22), zero)
         corner = {d: unfolded(level, got["corner"][d], 0) for d in CORNERS}
         wing = {
             (side, d): unfolded(level, got["wing"][side, d], 64 * side) for side in range(2) for d in range(8)
@@ -292,7 +293,7 @@
             p = plane - 2
             halves = []
             for half in range(n // 128):
-                value = jnp.zeros((c, 128), F32)
+                value = jnp.zeros((c, 128), BF)
                 for d in range(8):
                     if d * level.share // 128 != half:
                         continue
@@ -304,7 +305,7 @@
                     elif d in CORNERS:
                         piece, start = corner[d], 4 * p
                     else:
-                        piece = got["face"][d, p // level.per_tile].astype(F32)
+                        piece = got["face"][d, p // level.per_tile]
                         start = p % level.per_tile * level.share
                     value = jnp.where(which == base // level.share, ahead(piece, start - base), value)
                 halves.append(value)
@@ -313,11 +314,11 @@
         step = 4 if level is FINE else 5
         for first in range(0, level.planes, step):
             members = range(first, first + step)
-            rows = jnp.concatenate([halo(m) for m in members], axis=0).astype(BF)
-            placed = dot(rows, table[...])
+            rows = jnp.concatenate([halo(m) for m in members], axis=0)
+            placed = dot(rows, table[...]).astype(BF)
             for q, m in enumerate(members):
-                own = raw[:, m * n : (m + 1) * n].astype(F32)
-                full[:, m * n : (m + 1) * n] = (own + placed[q * c : (q + 1) * c]).astype(BF)
+                own = raw[:, m * n : (m + 1) * n]
+                full[:, m * n : (m + 1) * n] = own + placed[q * c : (q + 1) * c]
 
     def conv(level, src, weight, dst):
         c, n = level.width, level.lanes
@@ -327,11 +328,11 @@
         def one(g, carry):
             lanes = pl.ds(pl.multiple_of(g * width, width), width)
             for ib in range(c // 32):
-                rows = src[32 * ib : 32 * ib + 32, lanes].astype(F32)
+                rows = src[32 * ib : 32 * ib + 32, lanes]
                 for t in range(9):
                     shift = level.stride * (t // 3 - 1) + t % 3 - 1
                     top = 288 * ib + 32 * t
-                    cols[top : top + 32, :] = ahead(rows, shift).astype(BF)
+                    cols[top : top + 32, :] = ahead(rows, shift)
             sums[:, lanes] = dot(weight[...], cols[...])
             return carry
 
@@ -381,9 +382,13 @@
 
     zs = [zh, 1 - zh] if nzh == 2 else [zh]
 
-    def along_y(i):
-        for d, peer in enumerate(y_peers):
-            pass_on(at(zs[i], gy, gxx), ("y", i, d + 1), peer)
+    up, down = ny // 2, (ny - 1) // 2
+
+    def along_y(i, n):
+        if n < up:
+            pass_on(at(zs[i], (gy - n + ny) % ny, gxx), ("y+", i, n + 1), y_next)
+        if n < down:
+            pass_on(at(zs[i], (gy + n) % ny, gxx), ("y-", i, n + 1), y_last)
 
     def along_x(i, d, local):
         j = at(zs[i], (gy - d + ny) % ny, gxx)
@@ -395,7 +400,7 @@
 
     if nzh == 2:
         pass_on(yz, "z", z_peer)
-    along_y(0)
+    along_y(0, 0)
     along_x(0, 0, True)
 
     for n, name in enumerate(("efa", "efb", "dfa", "dfb")):
@@ -435,20 +440,28 @@
 
     lax.fori_loop(0, 27, block_rows, 0)
 
-    def step_y(i):
-        for d in sorted(range(1, ny), key=lambda d: min(d, ny - d)):
-            waiting["y", i, d].wait_recv()
-            along_x(i, d, False)
+    def step_y(i, n):
+        if i < nzh and n <= up:
+            waiting["y+", i, n].wait_recv()
+            if n <= down:
+                waiting["y-", i, n].wait_recv()
+            along_y(i, n)
+            along_x(i, n, False)
+            if n <= down:
+                along_x(i, ny - n, False)
 
     if nzh == 2:
         waiting["z"].wait_recv()
-        along_y(1)
+        along_y(1, 0)
         along_x(1, 0, False)
 
     full_x, mid_f = s["full_x"], s["mid_f"]
-    step_y(0)
+    for n, i in ((1, 0), (1, 1), (2, 0), (2, 1)):
+        step_y(i, n)
     unpack(FINE, raw_x, box_of("got_x"), full_x, sent_x)
     conv(FINE, full_x, s["wf"].at[0], mid_f)
+    step_y(0, 3)
+    step_y(1, 3)
     raw_e0 = s["raw_e0"]
     conv(FINE, mid_f, s["wf"].at[1], s["e0"])
 
@@ -458,14 +471,14 @@
         y, z = cells // level.stride - 2, cells % level.stride - 2
         inside = (y >= 0) & (y < level.extent) & (z >= 0) & (z < level.extent)
         for p in range(2, level.extent + 2):
-            value = src[:, p * n : (p + 1) * n].astype(F32)
-            raw[:, p * n : (p + 1) * n] = jnp.where(inside, value, 0.0).astype(BF)
+            value = src[:, p * n : (p + 1) * n]
+            raw[:, p * n : (p + 1) * n] = jnp.where(inside, value, jnp.zeros_like(value))
 
     keep_inside(FINE, s["e0"], raw_e0)
 
-    own = raw_e0[:, 512 : 14 * 256].astype(F32)
+    own = raw_e0[:, 512 : 14 * 256]
     for t in range(4):
-        moved = ahead(own, 16 * (t // 2) + t % 2).astype(BF)
+        moved = ahead(own, 16 * (t // 2) + t % 2)
         for j in range(6):
             for a in range(2):
                 top = 128 * a + 32 * t
@@ -480,8 +493,9 @@
         raw_h1[:, (j + 2) * 128 : (j + 3) * 128] = small[64 * j : 64 * j + 64]
     pack(MID, raw_h1, box_of("msg_h1"))
     sent_h1 = exchange(MID, raw_h1, box_of("msg_h1"), box_of("got_h1"), s["ss"].at[1], s["rs"].at[1])
-    if nzh == 2:
-        step_y(1)
+    for n in range(4, up + 1):
+        step_y(0, n)
+        step_y(1, n)
 
     full_m, mid_m = s["full_m"], s["mid_m"]
     unpack(MID, raw_h1, box_of("got_h1"), full_m, sent_h1)
@@ -490,9 +504,9 @@
     raw_e1 = s["raw_e1"]
     keep_inside(MID, s["e1"], raw_e1)
 
-    own = raw_e1[:, 256 : 8 * 128].astype(F32)
+    own = raw_e1[:, 256 : 8 * 128]
     for t in range(4):
-        moved = ahead(own, 10 * (t // 2) + t % 2).astype(BF)
+        moved = ahead(own, 10 * (t // 2) + t % 2)
         for j in range(3):
             for a in range(2):
                 for ib in range(2):
@@ -501,14 +515,14 @@
                         32 * ib : 32 * ib + 32, 128 * (2 * j + a) : 128 * (2 * j + a) + 128
                     ]
     wide = dot(s["wrm"][...], s["cols_rm"][...]).astype(BF)
-    cells = dot(wide, k["down_bottom"][...])
+    cells = dot(wide, k["down_bottom"][...]).astype(BF)
     which = group_of(64, 32)
-    tile = jnp.zeros((64, 128), F32)
+    tile = jnp.zeros((64, 128), BF)
     for q in range(4):
         tile = jnp.where(which == q, ahead(cells[64 * q : 64 * q + 64], -32 * q), tile)
-    s["msg_b"][...] = tile.astype(BF)
+    s["msg_b"][...] = tile
     got_b = s["got_b"]
-    got_b[13] = tile.astype(BF)
+    got_b[13] = tile
     sent_b = []
     for m, (a, b, c) in enumerate(ALL26):
         slot = 9 * (a + 1) + 3 * (b + 1) + c + 1
@@ -544,13 +558,13 @@
     for q in range(4):
         tiles = []
         for t in range(7):
-            tile = jnp.zeros((64, 128), F32)
+            tile = jnp.zeros((64, 128), BF)
             for b in range(4):
                 if 4 * t + b < 27:
                     tile = jnp.where(
-                        which == b, ahead(got_b[4 * t + b].astype(F32), 32 * (q - b)), tile
+                        which == b, ahead(got_b[4 * t + b], 32 * (q - b)), tile
                     )
-            tiles.append(tile.astype(BF))
+            tiles.append(tile)
         s["b0"][64 * q : 64 * q + 64, :] = dot(jnp.concatenate(tiles, axis=1), blocks[...]).astype(BF)
     for key, copy in waiting.items():
         if key[0] == "p":
@@ -562,10 +576,10 @@
         acc[:, :width] = jnp.zeros((256, width), F32)
 
         def one(kk, carry):
-            rows = src[pl.ds(pl.multiple_of(kk * 32, 32), 32), :].astype(F32)
+            rows = src[pl.ds(pl.multiple_of(kk * 32, 32), 32), :]
             for t in range(27):
                 shift = 81 * (t // 9) + 9 * (t // 3 % 3) + t % 3
-                cols_b[32 * t : 32 * t + 32, :width] = ahead(rows, shift)[:, :width].astype(BF)
+                cols_b[32 * t : 32 * t + 32, :width] = ahead(rows, shift)[:, :width]
             lhs = g_ref[m, kk % 2, pl.ds(pl.multiple_of(kk // 2 * 256, 256), 256), :]
             acc[:, :width] += dot(lhs, cols_b[:, :width])
             return carry
@@ -578,9 +592,9 @@
 
     full_e1 = s["full_e1"]
     unpack(MID, raw_e1, box_of("got_e1"), full_e1, sent_e1)
-    base = s["b2"][...].astype(F32)
+    base = s["b2"][...]
     for j in range(5):
-        spread = dot(ahead(base, 81 * j)[:, :128].astype(BF), k["up_mid"][...]).astype(BF)
+        spread = dot(ahead(base, 81 * j)[:, :128], k["up_mid"][...]).astype(BF)
         rows = jnp.concatenate([spread[:, 128 * q : 128 * q + 128] for q in range(4)], axis=0)
         risen = dot(s["wxm"][...], rows)
         for a in range(2):

time: 109 us -> 107 us (0.982)
  Pallas kernels: 107 us -> 105 us
    pallas_call x1, Pallas kernels: 107 us -> 105 us  [body(): pl.pallas_call(lambda *refs: kernel(ngx, nyz, place_of, *refs), name='une...]
where the time goes in v3:
time: 107 us
  Pallas kernels  105 us (98%)
  local copies, waits for them, and re-layouts  1.62 us (2%)
    pallas_call x1, Pallas kernels, body(): pl.pallas_call(lambda *refs: kernel(ngx, nyz, place_of, *refs), name='une...  105 us

profile of v3, /device:TPU:1, one launch (start us, length us, event | category | flops | bytes accessed | tf_op | source)
XLA Modules:
  0.0 106.7 jit_solution(15192158136924296339)
XLA Ops:
  0.0 105.1 %unet.1 = bf16[384,144]{1,0:T(8,128)(2,1)} custom-call(bf16[384,144]{1,0:T(8,128)(2,1)} %bitcast.11, bf16[32,864]{1,0:T(8,128)(2,1)} %refs_1_.1, bf16[32,864]{1,0:T(8,128)(2,1)} %refs_2_.1, bf16[64,256]{1,0:T(8,128)(2,1)} %refs_3_.1, bf16[64,1728]{1,0:T(8,128)(2,1)} %refs_4_.1, bf16[64,1728]{1,0:T(8,128)(2,1)} %refs_5_.1, bf16[256,512]{1,0:T(8,128)(2,1)} %refs_6_.1, ...), custom_call_target="tpu_custom_call" | custom-call | tf_op jit(solution)/shard_map/unet/pallas_call | solution.py:672
  105.1 1.6 %copy.30 = bf16[1,32,12,144]{3,1,2,0:T(8,128)(2,1)} copy(bf16[1,32,12,144]{3,1,2,0:T(8,128)(2,1)} %bitcast.10) | data formatting | bytes 221184

commit v4 on v3

--- a/solution.py
+++ b/solution.py
@@ -456,12 +456,12 @@
         along_x(1, 0, False)
 
     full_x, mid_f = s["full_x"], s["mid_f"]
-    for n, i in ((1, 0), (1, 1), (2, 0), (2, 1)):
+    for n, i in ((1, 0), (1, 1), (2, 0)):
         step_y(i, n)
     unpack(FINE, raw_x, box_of("got_x"), full_x, sent_x)
     conv(FINE, full_x, s["wf"].at[0], mid_f)
+    step_y(1, 2)
     step_y(0, 3)
-    step_y(1, 3)
     raw_e0 = s["raw_e0"]
     conv(FINE, mid_f, s["wf"].at[1], s["e0"])
 
@@ -493,6 +493,26 @@
         raw_h1[:, (j + 2) * 128 : (j + 3) * 128] = small[64 * j : 64 * j + 64]
     pack(MID, raw_h1, box_of("msg_h1"))
     sent_h1 = exchange(MID, raw_h1, box_of("msg_h1"), box_of("got_h1"), s["ss"].at[1], s["rs"].at[1])
+    order = [(i, d) for i in range(nzh) for d in sorted(range(ny), key=lambda d: min(d, ny - d))]
+    early = [(i, d) for i, d in order if min(d, ny - d) + i < 3]
+
+    def step_x(i, d):
+        y = (gy - d + ny) % ny
+        waiting["x+", i, d].wait_recv()
+        j = at(zs[i], y, (gxx + nx - 1) % nx)
+        if nx > 2 and i == 0:
+            pass_on(j, ("f", i, d), x_next)
+        pass_on(j, ("p", i, d, 1), partner)
+        if nx > 2:
+            waiting["x-", i, d].wait_recv()
+            j = at(zs[i], y, (gxx + 1) % nx)
+            if i == 1:
+                pass_on(j, ("f", i, d), x_last)
+            pass_on(j, ("p", i, d, 2), partner)
+
+    step_y(1, 3)
+    for i, d in early:
+        step_x(i, d)
     for n in range(4, up + 1):
         step_y(0, n)
         step_y(1, n)
@@ -532,20 +552,9 @@
     pack(MID, raw_e1, box_of("msg_e1"))
     sent_e1 = exchange(MID, raw_e1, box_of("msg_e1"), box_of("got_e1"), s["ss"].at[4], s["rs"].at[4])
 
-    order = [(i, d) for i in range(nzh) for d in sorted(range(ny), key=lambda d: min(d, ny - d))]
     for i, d in order:
-        y = (gy - d + ny) % ny
-        waiting["x+", i, d].wait_recv()
-        j = at(zs[i], y, (gxx + nx - 1) % nx)
-        if nx > 2 and i == 0:
-            pass_on(j, ("f", i, d), x_next)
-        pass_on(j, ("p", i, d, 1), partner)
-        if nx > 2:
-            waiting["x-", i, d].wait_recv()
-            j = at(zs[i], y, (gxx + 1) % nx)
-            if i == 1:
-                pass_on(j, ("f", i, d), x_last)
-            pass_on(j, ("p", i, d, 2), partner)
+        if (i, d) not in early:
+            step_x(i, d)
     pack(FINE, raw_e0, box_of("msg_e0"))
     sent_e0 = exchange(FINE, raw_e0, box_of("msg_e0"), box_of("got_e0"), s["ss"].at[2], s["rs"].at[2])
     if nx > 2:

time: 107 us -> 102 us (0.953)
  Pallas kernels: 105 us -> 101 us
    pallas_call x1, Pallas kernels: 105 us -> 101 us  [body(): pl.pallas_call(lambda *refs: kernel(ngx, nyz, place_of, *refs), name='une...]
where the time goes in v4:
time: 102 us
  Pallas kernels  101 us (99%)
  local copies, waits for them, and re-layouts  1.62 us (2%)
    pallas_call x1, Pallas kernels, body(): pl.pallas_call(lambda *refs: kernel(ngx, nyz, place_of, *refs), name='une...  101 us

profile of v4, /device:TPU:1, one launch (start us, length us, event | category | flops | bytes accessed | tf_op | source)
XLA Modules:
  0.0 102.2 jit_solution(11396822586347952199)
XLA Ops:
  0.0 100.6 %unet.1 = bf16[384,144]{1,0:T(8,128)(2,1)} custom-call(bf16[384,144]{1,0:T(8,128)(2,1)} %bitcast.11, bf16[32,864]{1,0:T(8,128)(2,1)} %refs_1_.1, bf16[32,864]{1,0:T(8,128)(2,1)} %refs_2_.1, bf16[64,256]{1,0:T(8,128)(2,1)} %refs_3_.1, bf16[64,1728]{1,0:T(8,128)(2,1)} %refs_4_.1, bf16[64,1728]{1,0:T(8,128)(2,1)} %refs_5_.1, bf16[256,512]{1,0:T(8,128)(2,1)} %refs_6_.1, ...), custom_call_target="tpu_custom_call" | custom-call | tf_op jit(solution)/shard_map/unet/pallas_call | solution.py:681
  100.6 1.6 %copy.30 = bf16[1,32,12,144]{3,1,2,0:T(8,128)(2,1)} copy(bf16[1,32,12,144]{3,1,2,0:T(8,128)(2,1)} %bitcast.10) | data formatting | bytes 221184
